TPU v7x, 128 devices: a whole 4x4x4 slice. The times are simulated.
128 devices in a mesh: shot: 8 (over y, core), rcv: 16 (over z, x).
Axes of the slice: x: 4, y: 4, z: 4, core: 2. Of those that a mesh axis runs over, the one named last changes fastest.
Arguments:
- traces: bfloat16 [8, 16, 1536, 2048], P('shot', 'rcv'), may hold values from -6 to 6
- trace_shot: int32 [8, 16, 1536], P('shot', 'rcv'), may hold values from 0 to 127, as said below
- trace_rcv: int32 [8, 16, 1536], P('shot', 'rcv'), may hold values from 0 to 127
- fold_count: int32 [8, 16], P('shot', 'rcv'), may hold values from 512 to 1536
Outputs:
- shot_terms: float32 [1024, 1024], P('shot')
- rcv_terms: float32 [2048, 1024], P('rcv')
Inputs may be any that keep to these rules, and one draw needn't show every extreme that they name: `trace_shot`: in every tile, slot k < 128 holds a distinct shot, and its receiver index equals its shot index, so every shot and receiver of the tile's blocks has a live trace there.
All inputs are finite; a program needn't handle non-finite values.
Results may differ from a plain program's by a relative error of at most 0.0072.
Values sent between devices are 32-bit elements; how exact they have to be, the bound alone decides.
A program may use at most 128 MiB of HBM per device.

v0:
```python
import math

import jax
import jax.numpy as jnp
from jax import lax
from jax.sharding import PartitionSpec as P

SHOT_DEV = 128
RCV_DEV = 128
SWEEPS = 3


def sent_to_all(x, axis):
    size = lax.axis_size(axis)
    return lax.all_to_all(jnp.broadcast_to(x[None], (size, *x.shape)), axis, 0, 0, tiled=True)


def of_everyone(x, axis):
    return sent_to_all(x, axis).sum(axis=0)


def side_by_side(arrays, axis, split_dim, concat_dim, along):
    widths = [a.shape[along] for a in arrays]
    both = jnp.concatenate(arrays, axis=along)
    result = lax.all_to_all(both, axis, split_axis=split_dim, concat_axis=concat_dim, tiled=True)
    return tuple(jnp.split(result, [sum(widths[:k]) for k in range(1, len(widths))], axis=along))


def in_one_piece(arrays, axis, dim, along):
    widths = [math.prod(a.shape[along:]) for a in arrays]
    both = jnp.concatenate(
        [a.reshape(*a.shape[:along], w) for a, w in zip(arrays, widths)], axis=along
    )
    result = lax.all_gather(both, axis, axis=dim, tiled=True)
    pieces = jnp.split(result, [sum(widths[:k]) for k in range(1, len(widths))], axis=along)
    return tuple(
        (b.reshape(*result.shape[:along], *a.shape[along:]) for a, b in zip(arrays, pieces))
    )


def dft_tables(samples_count, bins_count):
    index_n = jnp.arange(samples_count, dtype=jnp.int32)
    index_f = jnp.arange(bins_count, dtype=jnp.int32)
    product = index_n[:, None] * index_f[None, :] % samples_count
    angle_table = 2.0 * jnp.pi / samples_count * product.astype(jnp.float32)
    return (jnp.cos(angle_table).astype(jnp.bfloat16), jnp.sin(angle_table).astype(jnp.bfloat16))


def log_spectrum(trace_block, cos_table, sin_table, samples_count):
    real = jnp.dot(trace_block, cos_table, preferred_element_type=jnp.float32)
    imag = jnp.dot(trace_block, sin_table, preferred_element_type=jnp.float32)
    return jnp.log((real * real + imag * imag) / samples_count + 1e-06)


def shards(traces, trace_shot, trace_rcv, fold_count):
    slot_total = traces.shape[2]
    samples_count = traces.shape[3]
    bins_count = samples_count // 2
    tile_traces = traces[0, 0]
    live_count = fold_count[0, 0]
    cos_table, sin_table = dft_tables(samples_count, bins_count)
    alive = (jnp.arange(slot_total, dtype=jnp.int32) < live_count).astype(jnp.float32)
    onehot_shot = (
        trace_shot[0, 0][:, None] == jnp.arange(SHOT_DEV, dtype=jnp.int32)[None, :]
    ).astype(jnp.float32) * alive[:, None]
    onehot_rcv = (trace_rcv[0, 0][:, None] == jnp.arange(RCV_DEV, dtype=jnp.int32)[None, :]).astype(
        jnp.float32
    ) * alive[:, None]
    shot_count = of_everyone(jnp.sum(onehot_shot, axis=0), "rcv")
    rcv_count = lax.psum(jnp.sum(onehot_rcv, axis=0), "shot")
    spectra_log = log_spectrum(tile_traces, cos_table, sin_table, samples_count)
    shot_logs = jnp.dot(onehot_shot.T, spectra_log, precision=lax.Precision.HIGHEST)
    rcv_logs = jnp.dot(onehot_rcv.T, spectra_log, precision=lax.Precision.HIGHEST)
    pairs = jnp.dot(onehot_shot.T, onehot_rcv, precision=lax.Precision.HIGHEST)
    shot_blocks = lax.axis_size("shot")
    rcv_blocks = lax.axis_size("rcv")
    device_total = shot_blocks * rcv_blocks
    owned_bins = bins_count // device_total
    shot_parts, rcv_parts = side_by_side(
        (shot_logs[None], rcv_logs[None]), ("shot", "rcv"), 2, 0, 1
    )
    shot_whole = shot_parts.reshape(shot_blocks, rcv_blocks, SHOT_DEV, owned_bins).sum(axis=1)
    rcv_whole = rcv_parts.reshape(shot_blocks, rcv_blocks, RCV_DEV, owned_bins).sum(axis=0)
    pairs_every, shot_counts, rcv_counts = in_one_piece(
        (pairs[None], shot_count[None], rcv_count[None]), ("shot", "rcv"), 0, 2
    )
    pairs_every = pairs_every.reshape(shot_blocks, rcv_blocks, SHOT_DEV, RCV_DEV)
    shot_norm = shot_counts.reshape(shot_blocks, rcv_blocks, SHOT_DEV)[:, 0]
    rcv_norm = rcv_counts.reshape(shot_blocks, rcv_blocks, RCV_DEV)[0]
    rcv_local = jnp.zeros((rcv_blocks, RCV_DEV, owned_bins), jnp.float32)
    shot_local = jnp.zeros((shot_blocks, SHOT_DEV, owned_bins), jnp.float32)
    for iteration in range(SWEEPS):
        shot_total = shot_whole - jnp.einsum(
            "ijxy,jyf->ixf", pairs_every, rcv_local, precision=lax.Precision.HIGHEST
        )
        shot_local = shot_total / shot_norm[:, :, None]
        rcv_total = rcv_whole - jnp.einsum(
            "ijxy,ixf->jyf", pairs_every, shot_local, precision=lax.Precision.HIGHEST
        )
        rcv_local = rcv_total / rcv_norm[:, :, None]
    shot_send = jnp.broadcast_to(
        shot_local[:, None], (shot_blocks, rcv_blocks, SHOT_DEV, owned_bins)
    ).reshape(device_total, SHOT_DEV, owned_bins)
    rcv_send = jnp.broadcast_to(
        rcv_local[None], (shot_blocks, rcv_blocks, RCV_DEV, owned_bins)
    ).reshape(device_total, RCV_DEV, owned_bins)
    shot_back, rcv_back = side_by_side((shot_send, rcv_send), ("shot", "rcv"), 0, 2, 1)
    return (shot_back[0], rcv_back[0])


def solution(mesh):
    return jax.shard_map(
        shards,
        mesh=mesh,
        in_specs=(
            P("shot", "rcv", None, None),
            P("shot", "rcv", None),
            P("shot", "rcv", None),
            P("shot", "rcv"),
        ),
        out_specs=(P("shot", None), P("rcv", None)),
        check_vma=False,
    )
```

profile of v0, /device:TPU:1, one launch (start us, length us, event | category | flops | bytes accessed | tf_op | source)
XLA Modules:
  0.0 231.1 jit_solution(9240677281149231508)
XLA Ops:
  9.3 1.1 select_reduce_fusion.1
  10.9 8.4 %all-to-all-start.1 = ((f32[16,1,128]{2,1,0:T(1,128)}), f32[16,1,128]{2,1,0:T(1,128)S(1)}, u32[]{:S(2)}, u32[]{:S(2)}) async-start(f32[16,1,128]{2,1,0:T(1,128)} %broadcast_in_dim.17), calls=%async_computation.1 | async-start | bytes 16384 | tf_op jit(solution)/shard_map/all_to_all | solution.py:15
  19.4 2.3 fusion.27
  21.7 13.4 %psum.7 = f32[1,128,1]{1,2,0:T(1,128)S(1)} all-reduce(f32[1,128,1]{1,2,0:T(1,128)S(1)} %bitcast.152), channel_id=1, replica_groups=mesh['shot'=8,'rcv'=16] {'shot'}, use_global_device_ids=true, to_apply=%region_4.5 | all-reduce | flops 128 | bytes 1024 | tf_op jit(solution)/shard_map/psum | solution.py:70
  35.8 31.2 %sine_convert_fusion.4 = bf16[2048,1024]{1,0:T(8,128)(2,1)S(1)} fusion(), kind=kLoop, calls=%fused_computation.6.clone.clone.1 | loop fusion | flops 31457280 | bytes 4194304 | tf_op jit(solution)/shard_map/dot_general | solution.py:51
  67.1 31.0 %cosine_convert_fusion.4 = bf16[2048,1024]{1,0:T(8,128)(2,1)S(1)} fusion(), kind=kLoop, calls=%fused_computation.7.clone.clone.1 | loop fusion | flops 31457280 | bytes 4194304 | tf_op jit(solution)/shard_map/dot_general | solution.py:50
  98.1 8.7 %fusion.6 = f32[1024,1536]{1,0:T(8,128)} fusion(bf16[1,1,1536,2048]{3,2,1,0:T(8,128)(2,1)S(1)} %copy-done, bf16[2048,1024]{1,0:T(8,128)(2,1)S(1)} %sine_convert_fusion.4), kind=kOutput, calls=%fused_computation.11 | convolution fusion | flops 6442450944 | bytes 16777216 | tf_op jit(solution)/shard_map/dot_general | solution.py:51
  106.8 9.7 %add_log_fusion = f32[1024,1536]{1,0:T(8,128)S(1)} fusion(f32[1024,1536]{1,0:T(8,128)} %fusion.6, bf16[1,1,1536,2048]{3,2,1,0:T(8,128)(2,1)S(1)} %copy-done, bf16[2048,1024]{1,0:T(8,128)(2,1)S(1)} %cosine_convert_fusion.4), kind=kOutput, calls=%fused_computation.15 | convolution fusion | flops 6450315264 | bytes 23068672 | tf_op jit(solution)/shard_map/dot_general | solution.py:50
  116.5 5.8 %fusion.24 = f32[1,128,1024]{2,1,0:T(8,128)S(1)} fusion(f32[1024,1536]{1,0:T(8,128)S(1)} %add_log_fusion, s32[1536]{0:T(1024)S(1)} %reduce.2, f32[1536]{0:T(1024)S(1)} %fusion.60), kind=kOutput, calls=%fused_computation.26 | convolution fusion | flops 2416312320 | bytes 6828032 | tf_op jit(solution)/shard_map/dot_general | solution.py:73
  122.3 5.8 %fusion.21 = f32[1,128,1024]{2,1,0:T(8,128)S(1)} fusion(f32[1024,1536]{1,0:T(8,128)S(1)} %add_log_fusion, f32[1536]{0:T(1024)S(1)} %fusion.60, s32[1536]{0:T(1024)S(1)} %reduce.1), kind=kOutput, calls=%fused_computation.25 | convolution fusion | flops 2416312320 | bytes 6828032 | tf_op jit(solution)/shard_map/dot_general | solution.py:72
  128.2 0.8 copy.25
  128.9 28.2 %all_to_all.42 = f32[1,256,1024]{1,0,2:T(1,128)S(1)} all-to-all(f32[1,256,1024]{1,0,2:T(1,128)S(1)} %copy.25), channel_id=1, replica_groups=mesh['shot'=8,'rcv'=16] {'shot','rcv'}, dimensions={2} | all-to-all | bytes 2097152 | tf_op jit(solution)/shard_map/all_to_all | solution.py:25
  157.4 1.1 split.28
  158.5 4.0 %split.26 = f32[128,128,128]{1,2,0:T(8,128)S(1)} slice(f32[128,128,130]{1,2,0:T(8,128)} %all-gather.2.cloned.1.call-done), slice={[0:128], [0:128], [0:128]} | slice | bytes 16777216 | tf_op jit(solution)/shard_map/split | solution.py:35
  162.5 4.4 %fusion.42 = f32[8,128,8,1]{1,2,3,0:T(8,128)S(1)} fusion(f32[8,128,8]{1,2,0:T(8,128)S(1)} %bitcast_reduce_fusion, f32[8,16,128,128]{2,3,1,0:T(8,128)S(1)} %bitcast.131, f32[8,128]{1,0:T(8,128)S(1)} %bitcast.147), kind=kOutput, calls=%fused_computation.44 | convolution fusion | flops 201342976 | bytes 8458240 | tf_op jit(solution)/shard_map/ijxy,jyf->ixf/dot_general | solution.py:93
  166.9 0.9 slice.11
  167.7 7.2 %fusion.34 = f32[16,128,8,1]{1,2,0,3:T(8,128)S(1)} fusion(f32[16,128,8]{1,2,0:T(8,128)S(1)} %reduce_sum.49, f32[8,16,128,128]{2,3,1,0:T(8,128)S(1)} %bitcast.132, f32[8,128,8,1]{1,2,3,0:T(8,128)S(1)} %fusion.42, f32[16,128]{1,0:T(8,128)S(1)} %bitcast.143), kind=kOutput, calls=%fused_computation.33 | convolution fusion | flops 201359360 | bytes 8560640 | tf_op jit(solution)/shard_map/ijxy,ixf->jyf/dot_general | solution.py:97
  174.9 4.7 %fusion.45 = f32[8,128,8,1]{1,2,3,0:T(8,128)S(1)} fusion(f32[8,128,8]{1,2,0:T(8,128)S(1)} %bitcast_reduce_fusion, f32[8,16,128,128]{2,3,1,0:T(8,128)S(1)} %bitcast.133, f32[16,128,8,1]{1,2,0,3:T(8,128)S(1)} %fusion.34, f32[8,128]{1,0:T(8,128)S(1)} %bitcast.148), kind=kOutput, calls=%fused_computation.47 | convolution fusion | flops 201342976 | bytes 8523776 | tf_op jit(solution)/shard_map/ijxy,jyf->ixf/dot_general | solution.py:93
  179.6 7.2 %fusion.37 = f32[16,128,8,1]{1,2,0,3:T(8,128)S(1)} fusion(f32[16,128,8]{1,2,0:T(8,128)S(1)} %reduce_sum.49, f32[8,16,128,128]{2,3,1,0:T(8,128)S(1)} %bitcast.134, f32[8,128,8,1]{1,2,3,0:T(8,128)S(1)} %fusion.45, f32[16,128]{1,0:T(8,128)S(1)} %bitcast.144), kind=kOutput, calls=%fused_computation.36 | convolution fusion | flops 201359360 | bytes 8560640 | tf_op jit(solution)/shard_map/ijxy,ixf->jyf/dot_general | solution.py:97
  186.8 4.7 %fusion.47 = f32[8,128,8]{1,2,0:T(8,128)S(1)} fusion(f32[8,128,8]{1,2,0:T(8,128)S(1)} %bitcast_reduce_fusion, f32[8,16,128,128]{2,3,1,0:T(8,128)S(1)} %bitcast.135, f32[16,128,8,1]{1,2,0,3:T(8,128)S(1)} %fusion.37, f32[8,128]{1,0:T(8,128)S(1)} %bitcast.149), kind=kOutput, calls=%fused_computation.49 | convolution fusion | flops 201342976 | bytes 8523776 | tf_op jit(solution)/shard_map/ijxy,jyf->ixf/dot_general | solution.py:93
  191.5 7.2 %fusion.39 = f32[16,128,8]{1,2,0:T(8,128)S(1)} fusion(f32[16,128,8]{1,2,0:T(8,128)S(1)} %reduce_sum.49, f32[8,16,128,128]{2,3,1,0:T(8,128)S(1)} %bitcast.136, f32[8,128,8]{1,2,0:T(8,128)S(1)} %fusion.47, f32[16,128]{1,0:T(8,128)S(1)} %bitcast.145), kind=kOutput, calls=%fused_computation.38 | convolution fusion | flops 201359360 | bytes 8560640 | tf_op jit(solution)/shard_map/ijxy,ixf->jyf/dot_general | solution.py:97
  198.8 23.1 %all_to_all.43 = f32[128,256,8]{1,2,0:T(8,128)S(1)} all-to-all(f32[128,256,8]{1,2,0:T(8,128)S(1)} %pad_maximum_fusion.1), channel_id=1, replica_groups=mesh['shot'=8,'rcv'=16] {'shot','rcv'}, dimensions={0} | all-to-all | bytes 2097152 | tf_op jit(solution)/shard_map/all_to_all | solution.py:25
  222.0 1.0 copy.29
  223.0 1.0 copy.30
  (22 shorter events, 3.3 us)
Async XLA Ops:
  10.9 24.2 %all-to-all-start.1 = ((f32[16,1,128]{2,1,0:T(1,128)}), f32[16,1,128]{2,1,0:T(1,128)S(1)}, u32[]{:S(2)}, u32[]{:S(2)}) async-start(f32[16,1,128]{2,1,0:T(1,128)} %broadcast_in_dim.17), calls=%async_computation.1 | async-start | bytes 16384 | tf_op jit(solution)/shard_map/all_to_all | solution.py:15
  19.3 138.0 %all-gather.2.cloned.1.call-start = ((), (), s32[]{:S(2)}) async-start(), calls=%async_computation.3 | async-start | bytes 8982528 | tf_op jit(solution)/shard_map/all_gather | solution.py:34
  35.8 62.3 %copy-start = (bf16[1,1,1536,2048]{3,2,1,0:T(8,128)(2,1)S(1)}, bf16[1,1,1536,2048]{3,2,1,0:T(8,128)(2,1)}, u32[]{:S(2)}) copy-start(bf16[1,1,1536,2048]{3,2,1,0:T(8,128)(2,1)} %param.4) | copy-start | bytes 18874372
Sparse Core Ops, SparseCore 0:
  35.9 71.6 all-gather.1
where the time goes:
time: 234 us; the launch traced here: 231 us
  matrix products  67.6 us (29%)
  other arithmetic  65.6 us (28%)
  blocking collectives  64.7 us (28%)
  between operations  15.1 us (6%)
  local copies, waits for them, and re-layouts  9.54 us (4%)
  starting transfers between devices  8.46 us (4%)
    all_to_all x2, blocking collectives, side_by_side(): lax.all_to_all(both, axis, split_axis=split_dim, concat_axis=concat_dim,...  51.3 us
    dot_general x1, other arithmetic, log_spectrum(): imag = jnp.dot(trace_block, sin_table, preferred_element_type=jnp.float32)  31.2 us
    dot_general x1, other arithmetic, log_spectrum(): real = jnp.dot(trace_block, cos_table, preferred_element_type=jnp.float32)  31 us
    dot_general x3, matrix products, shards(): jnp.einsum('ijxy,ixf->jyf', pairs_every, shot_local, precision=lax.Precis...  21.5 us
    dot_general x3, matrix products, shards(): jnp.einsum('ijxy,jyf->ixf', pairs_every, rcv_local, precision=lax.Precisi...  13.8 us
    psum x1, blocking collectives, shards(): rcv_count = lax.psum(jnp.sum(onehot_rcv, axis=0), 'shot')  13.4 us
    dot_general x1, matrix products, log_spectrum(): real = jnp.dot(trace_block, cos_table, preferred_element_type=jnp.float32)  9.65 us
    dot_general x1, matrix products, log_spectrum(): imag = jnp.dot(trace_block, sin_table, preferred_element_type=jnp.float32)  8.73 us
  transfers between devices with their start and end apart: 2, of which 0 were waited for; matrix products, arithmetic and copies ran while one was open for 41% of the time, Pallas kernels for 0%

commit v1 on v0

v1 whole, which is shorter than its diff:
```python
import functools
import math

import jax
import jax.numpy as jnp
import numpy as np
from jax import lax
from jax.experimental import pallas as pl
from jax.experimental.pallas import tpu as pltpu
from jax.sharding import PartitionSpec as P

MESH = pl.DeviceIdType.MESH
VMEM = pltpu.VMEM
SWEEPS = 3
LANES = 128
CHIPS = 64
PLANE = 16
RINGS = 4
OWNED = 16
NT = (((1,), (1,)), ((), ()))
VMEM_LIMIT = 60 * 1024 * 1024


def phase_tables(samples):
    lane = np.arange(LANES)
    tile = np.arange(LANES)
    rows, turns = [], []
    for odd in range(2):
        angle = 2 * np.pi * ((8 * tile[:, None] * (2 * lane[None, :] + odd)) % samples) / samples
        rows.append(np.stack([np.cos(angle), np.sin(angle)]))
    sub = np.arange(8)
    for odd in range(2):
        for q in range(4):
            freq = 256 * q + 2 * lane + odd
            angle = 2 * np.pi * ((sub[:, None] * freq[None, :]) % samples) / samples
            turns.append(np.stack([np.cos(angle), np.sin(angle)]))
    return np.stack(rows).astype(np.float32), np.stack(turns).astype(np.float32)


def fill_table(table, rows_ref, turns_ref, odd, chunk):
    turn_c, turn_s = turns_ref[chunk, 0], turns_ref[chunk, 1]

    def step(m, carry):
        cos_rows, sin_rows = [], []
        for half in range(2):
            at = 2 * m + half
            rc = jnp.broadcast_to(rows_ref[odd, 0, pl.ds(at, 1), :], (8, LANES))
            rs = jnp.broadcast_to(rows_ref[odd, 1, pl.ds(at, 1), :], (8, LANES))
            cos_rows.append(rc * turn_c - rs * turn_s)
            sin_rows.append(rs * turn_c + rc * turn_s)
        at = pl.ds(pl.multiple_of(m * 16, 16), 16)
        table[at, :LANES] = jnp.concatenate(cos_rows, axis=0).astype(jnp.bfloat16)
        table[at, LANES:] = jnp.concatenate(sin_rows, axis=0).astype(jnp.bfloat16)
        return carry

    lax.fori_loop(0, 64, step, 0, unroll=8)


def one_hot(row, ids):
    wide = jnp.broadcast_to(row, (16, LANES)).astype(jnp.bfloat16)
    wide = jnp.concatenate([wide] * 8, axis=0)
    return jnp.where(wide == ids, jnp.ones_like(ids), jnp.zeros_like(ids))


def sublane_ids():
    return lax.broadcasted_iota(jnp.int32, (LANES, LANES), 0).astype(jnp.float32).astype(jnp.bfloat16)


def spectra_kernel(traces, index, rows_ref, turns_ref, out, held, folded, table, hot, sums, sem):
    slots, samples = held.shape
    half = samples // 2
    block = 256
    copies = []
    for b in range(slots // block):
        at = pl.ds(b * block, block)
        copy = pltpu.make_async_copy(traces.at[at], held.at[at], sem.at[b])
        copy.start()
        copies.append(copy)
    ids = sublane_ids()
    values = index[...].astype(jnp.float32)
    tiles = slots // LANES
    for r in range(tiles):
        hot[:LANES, r * LANES : (r + 1) * LANES] = one_hot(values[r : r + 1], ids)
        hot[LANES:, r * LANES : (r + 1) * LANES] = one_hot(values[tiles + r : tiles + r + 1], ids)
    for b, copy in enumerate(copies):
        copy.wait()
        at = pl.ds(b * block, block)
        low, high = held[at, :half].astype(jnp.float32), held[at, half:].astype(jnp.float32)
        folded[0, at, :] = (low + high).astype(jnp.bfloat16)
        folded[1, at, :] = (low - high).astype(jnp.bfloat16)

    def chunk_step(chunk, carry):
        odd = chunk // 4
        fill_table(table, rows_ref, turns_ref, odd, chunk)
        sums[...] = jnp.zeros_like(sums)
        for b in range(slots // 512):
            at = pl.ds(b * 512, 512)
            both = jnp.dot(folded[odd, at, :], table[...], preferred_element_type=jnp.float32)
            real, imag = both[:, :LANES], both[:, LANES:]
            logs = jnp.log((real * real + imag * imag) * (1.0 / samples) + 1e-6)
            top = logs.astype(jnp.bfloat16)
            rest = (logs - top.astype(jnp.float32)).astype(jnp.bfloat16)
            sums[...] += jnp.dot(
                hot[:, b * 512 : (b + 1) * 512],
                jnp.concatenate([top, rest], axis=1),
                preferred_element_type=jnp.float32,
            )
        total = (sums[:, :LANES] + sums[:, LANES:]).T
        at = pl.ds(chunk * 8, 8)
        out[at, :OWNED, :] = total[:, :LANES].reshape(8, OWNED, LANES)
        out[at, OWNED:, :] = total[:, LANES:].reshape(8, OWNED, LANES)
        return carry

    lax.fori_loop(0, 8, chunk_step, 0)


def my_place():
    shot, rcv = lax.axis_index("shot"), lax.axis_index("rcv")
    return shot // 2, lax.rem(shot, 2), rcv // 4, lax.rem(rcv, 4)


def other(k, place):
    y, core, z, x = place
    ty = lax.rem(y + k // 16, 4)
    tz = lax.rem(z + lax.rem(k // 4, 4), 4)
    tx = lax.rem(x + lax.rem(k, 4), 4)
    rcv = tz * 4 + tx
    return ty, rcv, ty * PLANE + rcv, (ty * 2 + core, rcv)


def greet(place, partner):
    barrier = pltpu.get_barrier_semaphore()

    def step(k, carry):
        pl.semaphore_signal(barrier, inc=1, device_id=other(k, place)[3], device_id_type=MESH)
        return carry

    lax.fori_loop(1, CHIPS, step, 0)
    if partner is not None:
        pl.semaphore_signal(barrier, inc=1, device_id=partner, device_id_type=MESH)
    pl.semaphore_wait(barrier, CHIPS - 1 + (partner is not None))


def exchange_kernel(index, blocks, index_all, shot_out, rcv_out, landed, index_landed, sems):
    place = my_place()
    y, core, z, x = place
    me = y * PLANE + z * 4 + x
    greet(place, None)

    def copies(k):
        ty, rcv, number, device = other(k, place)
        a = pltpu.make_async_remote_copy(
            index, index_landed.at[me], sems.at[0, number], sems.at[1, me], device_id=device, device_id_type=MESH
        )
        b = pltpu.make_async_remote_copy(
            blocks.at[number], landed.at[me], sems.at[2, number], sems.at[3, me], device_id=device, device_id_type=MESH
        )
        return a, b

    def arrivals(k):
        ty, rcv, number, device = other(k, place)
        a = pltpu.make_async_remote_copy(
            index, index_landed.at[number], sems.at[0, number], sems.at[1, number], device_id=device, device_id_type=MESH
        )
        b = pltpu.make_async_remote_copy(
            blocks.at[number], landed.at[number], sems.at[2, number], sems.at[3, number], device_id=device, device_id_type=MESH
        )
        return a, b

    def start(k, carry):
        for copy in copies(k):
            copy.start()
        return carry

    lax.fori_loop(1, CHIPS, start, 0)
    landed[me] = blocks[me]
    index_landed[me] = index[...]

    def finish(k, carry):
        for copy in arrivals(k):
            copy.wait()
        return carry

    lax.fori_loop(1, CHIPS, finish, 0)
    index_all[...] = index_landed[...]
    for b in range(RINGS):
        shot_out[:, b * LANES : (b + 1) * LANES] = landed[b * PLANE : (b + 1) * PLANE, :OWNED, :].sum(axis=0)
    whole = landed[:PLANE, OWNED:, :]
    for b in range(1, RINGS):
        whole = whole + landed[b * PLANE : (b + 1) * PLANE, OWNED:, :]
    for j in range(PLANE):
        rcv_out[:, j * LANES : (j + 1) * LANES] = whole[j]


def pairs_kernel(index_all, pairs, shot_count, rcv_count, hot, totals):
    tiles = index_all.shape[1] // 2
    ids = sublane_ids()
    totals[...] = jnp.zeros_like(totals)
    rcv_count[...] = jnp.zeros_like(rcv_count)

    def step(p, carry):
        block, j = p // PLANE, lax.rem(p, PLANE)
        values = index_all[p].astype(jnp.float32)
        shots = jnp.concatenate([one_hot(values[r : r + 1], ids) for r in range(tiles)], axis=1)
        rcvs = jnp.concatenate([one_hot(values[tiles + r : tiles + r + 1], ids) for r in range(tiles)], axis=1)
        pair = lax.dot_general(shots, rcvs, NT, preferred_element_type=jnp.float32)
        across = pl.ds(pl.multiple_of(j * LANES, LANES), LANES)
        pairs[pl.ds(pl.multiple_of(block * LANES, LANES), LANES), across] = pair.astype(jnp.bfloat16)
        totals[block] += pair
        rcv_count[:, across] += jnp.broadcast_to(pair.sum(axis=0, keepdims=True), (8, LANES))
        return carry

    lax.fori_loop(0, CHIPS, step, 0, unroll=2)
    for b in range(RINGS):
        row = totals[b].T.sum(axis=0, keepdims=True)
        shot_count[:, b * LANES : (b + 1) * LANES] = jnp.broadcast_to(row, (8, LANES))


def two_parts(value):
    top = value.astype(jnp.bfloat16)
    return jnp.concatenate([top, (value - top.astype(jnp.float32)).astype(jnp.bfloat16)], axis=0)


def sweeps_kernel(shot_logs, rcv_logs, pairs, shot_count, rcv_count, shot_out, rcv_out,
                  shot_send, rcv_send, shot_land, rcv_land, count_land, part_send, part_land, sems, part_sems):
    place = my_place()
    y, core, z, x = place
    me = y * PLANE + z * 4 + x
    partner = (y * 2 + 1 - core, z * 4 + x)
    greet(place, partner)

    def pair_copy(src, dst, n):
        return pltpu.make_async_remote_copy(
            src, dst, part_sems.at[0, n], part_sems.at[1, n], device_id=partner, device_id_type=MESH
        )

    count_copy = pair_copy(rcv_count, count_land, SWEEPS)
    count_copy.start()
    counts = shot_count[0:1, :]
    rcv_counts = None
    rcv_terms = None
    copies = [pair_copy(part_send.at[n], part_land.at[n], n) for n in range(SWEEPS)]

    def copy_to(src, dst, kind, k, mine):
        ty, rcv, number, device = other(k, place)
        at = me if mine else number
        source = src.at[ty] if kind == 0 else src.at[rcv]
        return pltpu.make_async_remote_copy(
            source, dst.at[at], sems.at[2 * kind, number], sems.at[2 * kind + 1, at], device_id=device, device_id_type=MESH
        )

    def send_all(src, dst, kind):
        def step(k, carry):
            copy_to(src, dst, kind, k, True).start()
            return carry

        lax.fori_loop(1, CHIPS, step, 0)

    for n in range(SWEEPS):
        if n == 0:
            shot_terms = shot_logs[...] / counts
        else:
            both = lax.dot_general(two_parts(rcv_terms), pairs[...], NT, preferred_element_type=jnp.float32)
            shot_terms = (shot_logs[...] - (both[:OWNED] + both[OWNED:])) / counts
        if n == SWEEPS - 1:
            for b in range(RINGS):
                shot_send[b] = shot_terms[:, b * LANES : (b + 1) * LANES]
            send_all(shot_send, shot_land, 0)
        both = jnp.dot(two_parts(shot_terms), pairs[...], preferred_element_type=jnp.float32)
        part = rcv_logs[...] - (both[:OWNED] + both[OWNED:])
        part_send[n] = part
        copies[n].start()
        if n == 0:
            count_copy.wait()
            rcv_counts = rcv_count[0:1, :] + count_land[0:1, :]
        copies[n].wait()
        rcv_terms = (part + part_land[n]) / rcv_counts
    for j in range(PLANE):
        rcv_send[j] = rcv_terms[:, j * LANES : (j + 1) * LANES]
    send_all(rcv_send, rcv_land, 1)
    shot_land[me] = shot_send[y]
    rcv_land[me] = rcv_send[z * 4 + x]

    def finish(k, carry):
        copy_to(shot_send, shot_land, 0, k, False).wait()
        copy_to(rcv_send, rcv_land, 1, k, False).wait()
        return carry

    lax.fori_loop(1, CHIPS, finish, 0)
    shot_out[...] = shot_land[...]
    rcv_out[...] = rcv_land[...]


def turn_kernel(shot_in, rcv_in, shot_out, rcv_out, order):
    half = order.shape[0] // 2
    for src, dst in ((shot_in, shot_out), (rcv_in, rcv_out)):
        order[pl.ds(0, half, stride=2), :] = src[:half]
        order[pl.ds(1, half, stride=2), :] = src[half:]
        dst[...] = order[...].T


def shards(traces, trace_shot, trace_rcv, fold_count):
    slots, samples = traces.shape[2:]
    bins = samples // 2
    tiles = slots // LANES
    rows_np, turns_np = phase_tables(samples)
    alive = jnp.arange(slots, dtype=jnp.int32).reshape(1, tiles, LANES) < fold_count[0, 0]
    index = jnp.stack([trace_shot[0, 0], trace_rcv[0, 0]]).reshape(2, tiles, LANES)
    index = jnp.where(alive, index, -1).reshape(2 * tiles, LANES)
    f32, bf16 = jnp.float32, jnp.bfloat16
    vmem = pl.BlockSpec(memory_space=VMEM)
    shape = jax.ShapeDtypeStruct
    blocks = pl.pallas_call(
        spectra_kernel,
        out_shape=shape((CHIPS, 2 * OWNED, LANES), f32),
        in_specs=[pl.BlockSpec(memory_space=pl.ANY), vmem, vmem, vmem],
        out_specs=vmem,
        scratch_shapes=[
            VMEM((slots, samples), bf16),
            VMEM((2, slots, samples // 2), bf16),
            VMEM((samples // 2, 2 * LANES), bf16),
            VMEM((2 * LANES, slots), bf16),
            VMEM((2 * LANES, 2 * LANES), f32),
            pltpu.SemaphoreType.DMA((slots // 256,)),
        ],
        compiler_params=pltpu.CompilerParams(vmem_limit_bytes=VMEM_LIMIT),
        name="spectra",
    )(traces[0, 0], index, jnp.asarray(rows_np), jnp.asarray(turns_np))
    index_all, shot_logs, rcv_logs = pl.pallas_call(
        exchange_kernel,
        out_shape=(
            shape((CHIPS, 2 * tiles, LANES), jnp.int32),
            shape((OWNED, RINGS * LANES), f32),
            shape((OWNED, PLANE * LANES), f32),
        ),
        in_specs=[vmem, vmem],
        out_specs=(vmem,) * 3,
        scratch_shapes=[
            VMEM((CHIPS, 2 * OWNED, LANES), f32),
            VMEM((CHIPS, 2 * tiles, LANES), jnp.int32),
            pltpu.SemaphoreType.DMA((4, CHIPS)),
        ],
        compiler_params=pltpu.CompilerParams(
            collective_id=0, has_side_effects=True, vmem_limit_bytes=VMEM_LIMIT
        ),
        name="exchange",
    )(index, blocks)
    pairs, shot_count, rcv_count = pl.pallas_call(
        pairs_kernel,
        out_shape=(
            shape((RINGS * LANES, PLANE * LANES), bf16),
            shape((8, RINGS * LANES), f32),
            shape((8, PLANE * LANES), f32),
        ),
        in_specs=[vmem],
        out_specs=(vmem,) * 3,
        scratch_shapes=[VMEM((8, LANES), f32), VMEM((RINGS, LANES, LANES), f32)],
        compiler_params=pltpu.CompilerParams(vmem_limit_bytes=VMEM_LIMIT),
        name="pairs",
    )(index_all)
    shot_got, rcv_got = pl.pallas_call(
        sweeps_kernel,
        out_shape=(shape((CHIPS, OWNED, LANES), f32), shape((CHIPS, OWNED, LANES), f32)),
        in_specs=[vmem] * 5,
        out_specs=(vmem,) * 2,
        scratch_shapes=[
            VMEM((RINGS, OWNED, LANES), f32),
            VMEM((PLANE, OWNED, LANES), f32),
            VMEM((CHIPS, OWNED, LANES), f32),
            VMEM((CHIPS, OWNED, LANES), f32),
            VMEM((8, PLANE * LANES), f32),
            VMEM((SWEEPS, OWNED, PLANE * LANES), f32),
            VMEM((SWEEPS, OWNED, PLANE * LANES), f32),
            pltpu.SemaphoreType.DMA((4, CHIPS)),
            pltpu.SemaphoreType.DMA((2, SWEEPS + 1)),
        ],
        compiler_params=pltpu.CompilerParams(
            collective_id=1, has_side_effects=True, vmem_limit_bytes=VMEM_LIMIT
        ),
        name="sweeps",
    )(shot_logs, rcv_logs, pairs, shot_count, rcv_count)
    return pl.pallas_call(
        turn_kernel,
        out_shape=(shape((LANES, bins), f32), shape((LANES, bins), f32)),
        in_specs=[vmem] * 2,
        out_specs=(vmem,) * 2,
        scratch_shapes=[VMEM((bins, LANES), f32)],
        compiler_params=pltpu.CompilerParams(vmem_limit_bytes=VMEM_LIMIT),
        name="turn",
    )(shot_got.reshape(bins, LANES), rcv_got.reshape(bins, LANES))


def solution(mesh):
    return jax.shard_map(
        shards,
        mesh=mesh,
        in_specs=(
            P("shot", "rcv", None, None),
            P("shot", "rcv", None),
            P("shot", "rcv", None),
            P("shot", "rcv"),
        ),
        out_specs=(P("shot", None), P("rcv", None)),
        check_vma=False,
    )
```

time: 234 us -> 117 us (0.50); the launches traced: 231 us -> 117 us
  Pallas kernels: 0 us -> 113 us
  matrix products: 67.6 us -> 0 us
  blocking collectives: 64.7 us -> 0 us
  other arithmetic: 65.6 us -> 1.45 us
  between operations: 15.1 us -> 1.32 us
  local copies, waits for them, and re-layouts: 9.54 us -> 0.6 us
  starting transfers between devices: 8.46 us -> 0 us
    pallas_call x0 -> x5, Pallas kernels: none -> 113 us  [the longest x1 42.8 us: shards(): pl.pallas_call(exchange_kernel, out_shape=(shape((CHIPS, 2 * tiles, LANES...]
    dot_general x11 -> x0, matrix products: 67.6 us -> none  [the longest x3 21.5 us: shards(): jnp.einsum('ijxy,ixf->jyf', pairs_every, shot_local, precision=lax.Precis...]
    dot_general x2 -> x0, other arithmetic: 62.2 us -> none  [the longest x1 31.2 us: log_spectrum(): imag = jnp.dot(trace_block, sin_table, preferred_element_type=jnp.float32)]
    all_to_all x2 -> x0, blocking collectives: 51.3 us -> none  [side_by_side(): lax.all_to_all(both, axis, split_axis=split_dim, concat_axis=concat_dim,...]
    psum x1 -> x0, blocking collectives: 13.4 us -> none  [shards(): rcv_count = lax.psum(jnp.sum(onehot_rcv, axis=0), 'shot')]
    all_to_all x1 -> x0, starting transfers between devices: 8.42 us -> none  [sent_to_all(): lax.all_to_all(jnp.broadcast_to(x[None], (size, *x.shape)), axis, 0, 0, t...]
    split x3 -> x0, local copies, waits for them, and re-layouts: 5.1 us -> none  [the longest x2 5.06 us: in_one_piece(): jnp.split(result, [sum(widths[:k]) for k in range(1, len(widths))], axis=...]
  transfers between devices with their start and end apart: 2 -> 0, of which waited for: 0 -> 0; matrix products, arithmetic and copies ran while one was open for 41% -> 0% of each run, Pallas kernels for 0% -> 0%
where the time goes in v1:
time: 117 us
  Pallas kernels  113 us (97%)
  other arithmetic  1.45 us (1%)
  between operations  1.32 us (1%)
    pallas_call x1, Pallas kernels, shards(): pl.pallas_call(exchange_kernel, out_shape=(shape((CHIPS, 2 * tiles, LANES...  42.8 us
    pallas_call x1, Pallas kernels, shards(): pl.pallas_call(sweeps_kernel, out_shape=(shape((CHIPS, OWNED, LANES), f32...  32.7 us
    pallas_call x1, Pallas kernels, shards(): pl.pallas_call(spectra_kernel, out_shape=shape((CHIPS, 2 * OWNED, LANES),...  20.4 us
    pallas_call x1, Pallas kernels, shards(): pl.pallas_call(pairs_kernel, out_shape=(shape((RINGS * LANES, PLANE * LAN...  15 us
    pallas_call x1, Pallas kernels, shards(): pl.pallas_call(turn_kernel, out_shape=(shape((LANES, bins), f32), shape((...  2.42 us

profile of v1, /device:TPU:1, one launch (start us, length us, event | category | flops | bytes accessed | tf_op | source)
XLA Modules:
  0.0 116.7 jit_solution(8604217222570566345)
XLA Ops:
  1.3 0.7 reduce
  2.0 0.7 reduce.1
  2.7 0.6 select_n.9.index
  3.3 20.4 %spectra.1.blocks = f32[64,32,128]{2,1,0:T(8,128)} custom-call(bf16[1536,2048]{1,0:T(8,128)(2,1)} %bitcast.7, s32[24,128]{1,0:T(8,128)} %select_n.9.index, f32[2,2,128,128]{3,2,1,0:T(8,128)} %constant.8.clone.rows_ref, f32[8,2,8,128]{3,2,1,0:T(8,128)} %constant.9.clone.turns_ref), custom_call_target="tpu_custom_call" | custom-call | tf_op jit(solution)/shard_map/spectra/pallas_call | solution.py:313
  23.8 42.8 %exchange.1 = (s32[64,24,128]{2,1,0:T(8,128)}, f32[16,512]{1,0:T(8,128)}, f32[16,2048]{1,0:T(8,128)}) custom-call(s32[24,128]{1,0:T(8,128)} %select_n.9.index, f32[64,32,128]{2,1,0:T(8,128)} %spectra.1.blocks), custom_call_target="tpu_custom_call" | custom-call | tf_op jit(solution)/shard_map/exchange/pallas_call | solution.py:329
  66.6 15.0 %pairs.1 = (bf16[512,2048]{1,0:T(8,128)(2,1)}, f32[8,512]{1,0:T(8,128)}, f32[8,2048]{1,0:T(8,128)}) custom-call(s32[64,24,128]{2,1,0:T(8,128)} %get-tuple-element.12.index_all), custom_call_target="tpu_custom_call" | custom-call | tf_op jit(solution)/shard_map/pairs/pallas_call | solution.py:348
  81.6 32.7 %sweeps.1 = (f32[64,16,128]{2,1,0:T(8,128)}, f32[64,16,128]{2,1,0:T(8,128)}) custom-call(f32[16,512]{1,0:T(8,128)} %get-tuple-element.10.shot_logs, f32[16,2048]{1,0:T(8,128)} %get-tuple-element.11.rcv_logs, bf16[512,2048]{1,0:T(8,128)(2,1)} %get-tuple-element.13.pairs, f32[8,512]{1,0:T(8,128)} %get-tuple-element.14.shot_count, ...), custom_call_target="tpu_custom_call" | custom-call | tf_op jit(solution)/shard_map/sweeps/pallas_call | solution.py:361
  114.3 2.4 %turn.1 = (f32[128,1024]{1,0:T(8,128)}, f32[128,1024]{1,0:T(8,128)}) custom-call(f32[1024,128]{1,0:T(8,128)} %bitcast.8, f32[1024,128]{1,0:T(8,128)} %bitcast.9), custom_call_target="tpu_custom_call" | custom-call | tf_op jit(solution)/shard_map/turn/pallas_call | solution.py:382
  (2 shorter events, 0.0 us)

commit v2 on v1

v2 whole, which is shorter than its diff:
```python
import functools
import math

import jax
import jax.numpy as jnp
import numpy as np
from jax import lax
from jax.experimental import pallas as pl
from jax.experimental.pallas import tpu as pltpu
from jax.sharding import PartitionSpec as P

MESH = pl.DeviceIdType.MESH
VMEM = pltpu.VMEM
SWEEPS = 3
LANES = 128
CHIPS = 64
PLANE = 16
RINGS = 4
OWNED = 16
NT = (((1,), (1,)), ((), ()))
VMEM_LIMIT = 60 * 1024 * 1024


def phase_tables(samples):
    lane = np.arange(LANES)
    tile = np.arange(LANES)
    rows, turns = [], []
    for odd in range(2):
        angle = 2 * np.pi * ((8 * tile[:, None] * (2 * lane[None, :] + odd)) % samples) / samples
        rows.append(np.stack([np.cos(angle), np.sin(angle)]))
    sub = np.arange(8)
    for odd in range(2):
        for q in range(4):
            freq = 256 * q + 2 * lane + odd
            angle = 2 * np.pi * ((sub[:, None] * freq[None, :]) % samples) / samples
            turns.append(np.stack([np.cos(angle), np.sin(angle)]))
    return np.stack(rows).astype(np.float32), np.stack(turns).astype(np.float32)


def fill_table(table, rows_ref, turns_ref, odd, chunk):
    turn_c, turn_s = turns_ref[chunk, 0], turns_ref[chunk, 1]
    half = table.shape[0] // 2
    sign = (1 - 2 * odd).astype(jnp.float32)

    def step(m, carry):
        cos_rows, sin_rows = [], []
        for part in range(2):
            at = 2 * m + part
            rc = jnp.broadcast_to(rows_ref[odd, 0, pl.ds(at, 1), :], (8, LANES))
            rs = jnp.broadcast_to(rows_ref[odd, 1, pl.ds(at, 1), :], (8, LANES))
            cos_rows.append(rc * turn_c - rs * turn_s)
            sin_rows.append(rs * turn_c + rc * turn_s)
        both = jnp.concatenate([jnp.concatenate(cos_rows, axis=0), jnp.concatenate(sin_rows, axis=0)], axis=1)
        start = pl.multiple_of(m * 16, 16)
        table[pl.ds(start, 16), :] = both.astype(jnp.bfloat16)
        table[pl.ds(start + half, 16), :] = (both * sign).astype(jnp.bfloat16)
        return carry

    lax.fori_loop(0, 64, step, 0, unroll=8)


def one_hot(row, ids):
    wide = jnp.broadcast_to(row, (16, LANES)).astype(jnp.bfloat16)
    wide = jnp.concatenate([wide] * 8, axis=0)
    return jnp.where(wide == ids, jnp.ones_like(ids), jnp.zeros_like(ids))


def sublane_ids():
    return lax.broadcasted_iota(jnp.int32, (LANES, LANES), 0).astype(jnp.float32).astype(jnp.bfloat16)


def my_place():
    shot, rcv = lax.axis_index("shot"), lax.axis_index("rcv")
    return shot // 2, lax.rem(shot, 2), rcv // 4, lax.rem(rcv, 4)


def other(k, place):
    y, core, z, x = place
    ty = lax.rem(y + k // 16, 4)
    tz = lax.rem(z + lax.rem(k // 4, 4), 4)
    tx = lax.rem(x + lax.rem(k, 4), 4)
    rcv = tz * 4 + tx
    return ty, rcv, ty * PLANE + rcv, (ty * 2 + core, rcv)


def device_of(number, core):
    return (number // PLANE) * 2 + core, lax.rem(number, PLANE)


def greet(place, partner):
    barrier = pltpu.get_barrier_semaphore()

    def step(k, carry):
        pl.semaphore_signal(barrier, inc=1, device_id=other(k, place)[3], device_id_type=MESH)
        return carry

    lax.fori_loop(1, CHIPS, step, 0)
    pl.semaphore_signal(barrier, inc=1, device_id=partner, device_id_type=MESH)
    return lambda: pl.semaphore_wait(barrier, CHIPS)


def two_parts(value, axis):
    top = value.astype(jnp.bfloat16)
    return jnp.concatenate([top, (value - top.astype(jnp.float32)).astype(jnp.bfloat16)], axis=axis)


def main_kernel(traces, index, rows_ref, turns_ref, shot_out, rcv_out,
                held, table, hot, blocks, landed, index_landed,
                pairs, totals, rcv_count, count_land,
                shot_send, rcv_send, shot_land, rcv_land, part_send, part_land,
                trace_sem, sems, term_sems, part_sems):
    place = my_place()
    y, core, z, x = place
    mine = z * 4 + x
    me = y * PLANE + mine
    partner = (y * 2 + 1 - core, mine)
    slots, samples = held.shape
    tiles = slots // LANES

    all_here = greet(place, partner)
    block = 512
    loads = [
        pltpu.make_async_copy(traces.at[pl.ds(b * block, block)], held.at[pl.ds(b * block, block)], trace_sem.at[b])
        for b in range(slots // block)
    ]
    for load in loads:
        load.start()
    ids = sublane_ids()
    values = index[...].astype(jnp.float32)
    for r in range(tiles):
        hot[:LANES, r * LANES : (r + 1) * LANES] = one_hot(values[r : r + 1], ids)
        hot[LANES:, r * LANES : (r + 1) * LANES] = one_hot(values[tiles + r : tiles + r + 1], ids)
    index_landed[me] = index[...]
    all_here()

    def index_copy(k, slot):
        number, device = other(k, place)[2:]
        return pltpu.make_async_remote_copy(
            index, index_landed.at[number if slot is None else slot], sems.at[0, number],
            sems.at[1, number if slot is None else slot], device_id=device, device_id_type=MESH
        )

    def block_copy(number, slot):
        return pltpu.make_async_remote_copy(
            blocks.at[number], landed.at[slot], sems.at[2, number], sems.at[3, slot],
            device_id=device_of(number, core), device_id_type=MESH
        )

    def send_index(k, carry):
        index_copy(k, me).start()
        return carry

    lax.fori_loop(1, CHIPS, send_index, 0)
    for load in loads:
        load.wait()

    def chunk_step(t, carry):
        chunk = lax.rem(t + me, 8)
        fill_table(table, rows_ref, turns_ref, chunk // 4, chunk)
        total = None
        for b in range(slots // block):
            both = jnp.dot(held[b * block : (b + 1) * block], table[...], preferred_element_type=jnp.float32)
            real, imag = both[:, :LANES], both[:, LANES:]
            logs = jnp.log((real * real + imag * imag) * (1.0 / samples) + 1e-6)
            part = jnp.dot(
                hot[:, b * block : (b + 1) * block], two_parts(logs, 1), preferred_element_type=jnp.float32
            )
            total = part if total is None else total + part
        total = (total[:, :LANES] + total[:, LANES:]).T
        at = pl.ds(chunk * 8, 8)
        blocks[at, :OWNED, :] = total[:, :LANES].reshape(8, OWNED, LANES)
        blocks[at, OWNED:, :] = total[:, LANES:].reshape(8, OWNED, LANES)

        def send(n, inner):
            number = chunk * 8 + n

            @pl.when(number != me)
            def _():
                block_copy(number, me).start()

            return inner

        lax.fori_loop(0, 8, send, 0)
        return carry

    lax.fori_loop(0, 8, chunk_step, 0)
    landed[me] = blocks[me]

    totals[...] = jnp.zeros_like(totals)
    rcv_count[...] = jnp.zeros_like(rcv_count)

    def pair_step(number):
        ty, j = number // PLANE, lax.rem(number, PLANE)
        values = index_landed[number].astype(jnp.float32)
        shots = jnp.concatenate([one_hot(values[r : r + 1], ids) for r in range(tiles)], axis=1)
        rcvs = jnp.concatenate([one_hot(values[tiles + r : tiles + r + 1], ids) for r in range(tiles)], axis=1)
        pair = lax.dot_general(shots, rcvs, NT, preferred_element_type=jnp.float32)
        across = pl.ds(pl.multiple_of(j * LANES, LANES), LANES)
        pairs[pl.ds(pl.multiple_of(ty * LANES, LANES), LANES), across] = pair.astype(jnp.bfloat16)
        totals[ty] += pair
        rcv_count[:, across] += jnp.broadcast_to(pair.sum(axis=0, keepdims=True), (8, LANES))

    pair_step(me)

    def pair_loop(k, carry):
        index_copy(k, None).wait()
        pair_step(other(k, place)[2])
        return carry

    lax.fori_loop(1, CHIPS, pair_loop, 0)

    def pair_copy(src, dst, n):
        return pltpu.make_async_remote_copy(
            src, dst, part_sems.at[0, n], part_sems.at[1, n], device_id=partner, device_id_type=MESH
        )

    count_copy = pair_copy(rcv_count, count_land, SWEEPS)
    count_copy.start()
    counts = jnp.concatenate([totals[b].T.sum(axis=0, keepdims=True) for b in range(RINGS)], axis=1)

    def block_wait(k, carry):
        number = other(k, place)[2]
        block_copy(number, number).wait()
        return carry

    lax.fori_loop(1, CHIPS, block_wait, 0)
    shot_logs = jnp.concatenate(
        [landed[b * PLANE : (b + 1) * PLANE, :OWNED, :].sum(axis=0) for b in range(RINGS)], axis=1
    )
    rcv_logs = landed[:PLANE, OWNED:, :]
    for b in range(1, RINGS):
        rcv_logs = rcv_logs + landed[b * PLANE : (b + 1) * PLANE, OWNED:, :]
    rcv_logs = jnp.concatenate([rcv_logs[j] for j in range(PLANE)], axis=1)
    count_copy.wait()
    rcv_counts = rcv_count[0:1, :] + count_land[0:1, :]
    copies = [pair_copy(part_send.at[n], part_land.at[n], n) for n in range(SWEEPS)]

    def copy_to(src, dst, kind, k, sending):
        ty, rcv, number, device = other(k, place)
        at = me if sending else number
        source = src.at[ty] if kind == 0 else src.at[rcv]
        return pltpu.make_async_remote_copy(
            source, dst.at[at], term_sems.at[2 * kind, number], term_sems.at[2 * kind + 1, at],
            device_id=device, device_id_type=MESH
        )

    def send_all(src, dst, kind):
        def step(k, carry):
            copy_to(src, dst, kind, k, True).start()
            return carry

        lax.fori_loop(1, CHIPS, step, 0)

    rcv_terms = None
    for n in range(SWEEPS):
        if n == 0:
            shot_terms = shot_logs / counts
        else:
            both = lax.dot_general(two_parts(rcv_terms, 0), pairs[...], NT, preferred_element_type=jnp.float32)
            shot_terms = (shot_logs - (both[:OWNED] + both[OWNED:])) / counts
        if n == SWEEPS - 1:
            for b in range(RINGS):
                shot_send[b] = shot_terms[:, b * LANES : (b + 1) * LANES]
            send_all(shot_send, shot_land, 0)
        both = jnp.dot(two_parts(shot_terms, 0), pairs[...], preferred_element_type=jnp.float32)
        part = rcv_logs - (both[:OWNED] + both[OWNED:])
        part_send[n] = part
        copies[n].start()
        copies[n].wait()
        rcv_terms = (part + part_land[n]) / rcv_counts
    for j in range(PLANE):
        rcv_send[j] = rcv_terms[:, j * LANES : (j + 1) * LANES]
    send_all(rcv_send, rcv_land, 1)
    shot_land[me] = shot_send[y]
    rcv_land[me] = rcv_send[mine]

    def finish(k, carry):
        copy_to(shot_send, shot_land, 0, k, False).wait()
        copy_to(rcv_send, rcv_land, 1, k, False).wait()
        return carry

    lax.fori_loop(1, CHIPS, finish, 0)
    shot_out[...] = shot_land[...]
    rcv_out[...] = rcv_land[...]


def turn_kernel(shot_in, rcv_in, shot_out, rcv_out, order):
    half = order.shape[0] // 2
    for src, dst in ((shot_in, shot_out), (rcv_in, rcv_out)):
        order[pl.ds(0, half, stride=2), :] = src[:half]
        order[pl.ds(1, half, stride=2), :] = src[half:]
        dst[...] = order[...].T


def shards(traces, trace_shot, trace_rcv, fold_count):
    slots, samples = traces.shape[2:]
    bins = samples // 2
    tiles = slots // LANES
    rows_np, turns_np = phase_tables(samples)
    alive = jnp.arange(slots, dtype=jnp.int32).reshape(1, tiles, LANES) < fold_count[0, 0]
    index = jnp.stack([trace_shot[0, 0], trace_rcv[0, 0]]).reshape(2, tiles, LANES)
    index = jnp.where(alive, index, -1).reshape(2 * tiles, LANES)
    f32, bf16 = jnp.float32, jnp.bfloat16
    vmem = pl.BlockSpec(memory_space=VMEM)
    shape = jax.ShapeDtypeStruct
    shot_got, rcv_got = pl.pallas_call(
        main_kernel,
        out_shape=(shape((CHIPS, OWNED, LANES), f32), shape((CHIPS, OWNED, LANES), f32)),
        in_specs=[pl.BlockSpec(memory_space=pl.ANY), vmem, vmem, vmem],
        out_specs=(vmem,) * 2,
        scratch_shapes=[
            VMEM((slots, samples), bf16),
            VMEM((samples, 2 * LANES), bf16),
            VMEM((2 * LANES, slots), bf16),
            VMEM((CHIPS, 2 * OWNED, LANES), f32),
            VMEM((CHIPS, 2 * OWNED, LANES), f32),
            VMEM((CHIPS, 2 * tiles, LANES), jnp.int32),
            VMEM((RINGS * LANES, PLANE * LANES), bf16),
            VMEM((RINGS, LANES, LANES), f32),
            VMEM((8, PLANE * LANES), f32),
            VMEM((8, PLANE * LANES), f32),
            VMEM((RINGS, OWNED, LANES), f32),
            VMEM((PLANE, OWNED, LANES), f32),
            VMEM((CHIPS, OWNED, LANES), f32),
            VMEM((CHIPS, OWNED, LANES), f32),
            VMEM((SWEEPS, OWNED, PLANE * LANES), f32),
            VMEM((SWEEPS, OWNED, PLANE * LANES), f32),
            pltpu.SemaphoreType.DMA((slots // 512,)),
            pltpu.SemaphoreType.DMA((4, CHIPS)),
            pltpu.SemaphoreType.DMA((4, CHIPS)),
            pltpu.SemaphoreType.DMA((2, SWEEPS + 1)),
        ],
        compiler_params=pltpu.CompilerParams(
            collective_id=0, has_side_effects=True, vmem_limit_bytes=VMEM_LIMIT
        ),
        name="decompose",
    )(traces[0, 0], index, jnp.asarray(rows_np), jnp.asarray(turns_np))
    return pl.pallas_call(
        turn_kernel,
        out_shape=(shape((LANES, bins), f32), shape((LANES, bins), f32)),
        in_specs=[vmem] * 2,
        out_specs=(vmem,) * 2,
        scratch_shapes=[VMEM((bins, LANES), f32)],
        compiler_params=pltpu.CompilerParams(vmem_limit_bytes=VMEM_LIMIT),
        name="turn",
    )(shot_got.reshape(bins, LANES), rcv_got.reshape(bins, LANES))


def solution(mesh):
    return jax.shard_map(
        shards,
        mesh=mesh,
        in_specs=(
            P("shot", "rcv", None, None),
            P("shot", "rcv", None),
            P("shot", "rcv", None),
            P("shot", "rcv"),
        ),
        out_specs=(P("shot", None), P("rcv", None)),
        check_vma=False,
    )
```

time: 117 us -> 86.1 us (0.74)
  Pallas kernels: 113 us -> 82.3 us
    pallas_call x4 -> x1, Pallas kernels: 111 us -> 79.9 us  [shards(): pl.pallas_call(main_kernel, out_shape=(shape((CHIPS, OWNED, LANES), f32),...]
where the time goes in v2:
time: 86.1 us; the launch traced here: 85.6 us
  Pallas kernels  82.3 us (96%)
  other arithmetic  1.45 us (2%)
  between operations  1.3 us (2%)
    pallas_call x1, Pallas kernels, shards(): pl.pallas_call(main_kernel, out_shape=(shape((CHIPS, OWNED, LANES), f32),...  79.9 us
    pallas_call x1, Pallas kernels, shards(): pl.pallas_call(turn_kernel, out_shape=(shape((LANES, bins), f32), shape((...  2.42 us

profile of v2, /device:TPU:1, one launch (start us, length us, event | category | flops | bytes accessed | tf_op | source)
XLA Modules:
  0.0 85.6 jit_solution(9667160153245387368)
XLA Ops:
  1.3 0.7 reduce
  2.0 0.7 reduce.1
  2.7 0.6 select_n.9.index
  3.3 79.9 %decompose.1 = (f32[64,16,128]{2,1,0:T(8,128)}, f32[64,16,128]{2,1,0:T(8,128)}) custom-call(bf16[1536,2048]{1,0:T(8,128)(2,1)} %bitcast.7, s32[24,128]{1,0:T(8,128)} %select_n.9.index, f32[2,2,128,128]{3,2,1,0:T(8,128)} %constant.8.clone.rows_ref, f32[8,2,8,128]{3,2,1,0:T(8,128)} %constant.9.clone.turns_ref), custom_call_target="tpu_custom_call" | custom-call | tf_op jit(solution)/shard_map/decompose/pallas_call | solution.py:306
  83.2 2.4 %turn.1 = (f32[128,1024]{1,0:T(8,128)}, f32[128,1024]{1,0:T(8,128)}) custom-call(f32[1024,128]{1,0:T(8,128)} %bitcast.8, f32[1024,128]{1,0:T(8,128)} %bitcast.9), custom_call_target="tpu_custom_call" | custom-call | tf_op jit(solution)/shard_map/turn/pallas_call | solution.py:338
  (2 shorter events, 0.0 us)

commit v3 on v2

--- a/solution.py
+++ b/solution.py
@@ -23,40 +23,43 @@
 
 def phase_tables(samples):
     lane = np.arange(LANES)
-    tile = np.arange(LANES)
-    rows, turns = [], []
-    for odd in range(2):
-        angle = 2 * np.pi * ((8 * tile[:, None] * (2 * lane[None, :] + odd)) % samples) / samples
-        rows.append(np.stack([np.cos(angle), np.sin(angle)]))
-    sub = np.arange(8)
-    for odd in range(2):
-        for q in range(4):
-            freq = 256 * q + 2 * lane + odd
-            angle = 2 * np.pi * ((sub[:, None] * freq[None, :]) % samples) / samples
-            turns.append(np.stack([np.cos(angle), np.sin(angle)]))
-    return np.stack(rows).astype(np.float32), np.stack(turns).astype(np.float32)
-
-
-def fill_table(table, rows_ref, turns_ref, odd, chunk):
-    turn_c, turn_s = turns_ref[chunk, 0], turns_ref[chunk, 1]
-    half = table.shape[0] // 2
-    sign = (1 - 2 * odd).astype(jnp.float32)
+    wave = lambda steps: np.stack([g(2 * np.pi * (steps % samples) / samples) for g in (np.cos, np.sin)])
+    rows = wave(16 * lane[:, None] * lane[None, :])
+    sub = np.arange(8)[:, None]
+    turns = [[wave((2 * sub + odd) * (LANES * q + lane[None, :])) for odd in range(2)] for q in range(4)]
+    return rows.astype(np.float32), np.array(turns).astype(np.float32)
+
+
+def fill_tables(table, rows_ref, turns_ref, q):
+    turns = [[turns_ref[q, odd, part] for part in range(2)] for odd in range(2)]
 
     def step(m, carry):
-        cos_rows, sin_rows = [], []
+        tops = [[], []]
         for part in range(2):
             at = 2 * m + part
-            rc = jnp.broadcast_to(rows_ref[odd, 0, pl.ds(at, 1), :], (8, LANES))
-            rs = jnp.broadcast_to(rows_ref[odd, 1, pl.ds(at, 1), :], (8, LANES))
-            cos_rows.append(rc * turn_c - rs * turn_s)
-            sin_rows.append(rs * turn_c + rc * turn_s)
-        both = jnp.concatenate([jnp.concatenate(cos_rows, axis=0), jnp.concatenate(sin_rows, axis=0)], axis=1)
-        start = pl.multiple_of(m * 16, 16)
-        table[pl.ds(start, 16), :] = both.astype(jnp.bfloat16)
-        table[pl.ds(start + half, 16), :] = (both * sign).astype(jnp.bfloat16)
+            rc = jnp.broadcast_to(rows_ref[0, pl.ds(at, 1), :], (8, LANES))
+            rs = jnp.broadcast_to(rows_ref[1, pl.ds(at, 1), :], (8, LANES))
+            for odd in range(2):
+                turn_c, turn_s = turns[odd]
+                tops[odd].append(jnp.concatenate([rc * turn_c - rs * turn_s, rs * turn_c + rc * turn_s], axis=1))
+        at = pl.ds(pl.multiple_of(m * 16, 16), 16)
+        for odd in range(2):
+            table[odd, at, :] = jnp.concatenate(tops[odd], axis=0).astype(jnp.bfloat16)
         return carry
 
     lax.fori_loop(0, 64, step, 0, unroll=8)
+
+    @pl.when(q == 0)
+    def _():
+        first = lax.broadcasted_iota(jnp.int32, (8, LANES), 1) == 0
+        flip = 1.0 - 2.0 * lax.rem(lax.broadcasted_iota(jnp.int32, (8, LANES), 0), 2).astype(jnp.float32)
+        flip = jnp.concatenate([flip, flip], axis=0)
+        first = jnp.concatenate([first, first], axis=0)
+        for odd in range(2):
+            for m in range(64):
+                at = pl.ds(m * 16, 16)
+                old = table[odd, at, LANES:].astype(jnp.float32)
+                table[odd, at, LANES:] = jnp.where(first, flip, old).astype(jnp.bfloat16)
 
 
 def one_hot(row, ids):
@@ -104,8 +107,8 @@
     return jnp.concatenate([top, (value - top.astype(jnp.float32)).astype(jnp.bfloat16)], axis=axis)
 
 
-def main_kernel(traces, index, rows_ref, turns_ref, shot_out, rcv_out,
-                held, table, hot, blocks, landed, index_landed,
+def main_kernel(fold, trace_shot, trace_rcv, traces, rows_ref, turns_ref, shot_out, rcv_out,
+                index, held, halves, table, hot, blocks, landed, index_landed,
                 pairs, totals, rcv_count, count_land,
                 shot_send, rcv_send, shot_land, rcv_land, part_send, part_land,
                 trace_sem, sems, term_sems, part_sems):
@@ -125,13 +128,31 @@
     ]
     for load in loads:
         load.start()
+    lane = lax.broadcasted_iota(jnp.int32, (1, LANES), 1)
+    for r in range(tiles):
+        live = lane + r * LANES < fold[0, 0]
+        at = slice(r * LANES, (r + 1) * LANES)
+        index[r : r + 1, :] = jnp.where(live, trace_shot[:, at], -1)
+        index[tiles + r : tiles + r + 1, :] = jnp.where(live, trace_rcv[:, at], -1)
     ids = sublane_ids()
     values = index[...].astype(jnp.float32)
     for r in range(tiles):
         hot[:LANES, r * LANES : (r + 1) * LANES] = one_hot(values[r : r + 1], ids)
         hot[LANES:, r * LANES : (r + 1) * LANES] = one_hot(values[tiles + r : tiles + r + 1], ids)
     index_landed[me] = index[...]
-    all_here()
+    wide = 2 * LANES
+    rank = lax.broadcasted_iota(jnp.int32, (wide, wide), 0)
+    spot = lax.broadcasted_iota(jnp.int32, (wide, wide), 1)
+    wanted = jnp.where(spot < LANES, 2 * spot, 2 * (spot - LANES) + 1)
+    split = jnp.where(rank == wanted, 1.0, 0.0).astype(jnp.bfloat16)
+    for b, load in enumerate(loads):
+        load.wait()
+        for n in range(samples // wide):
+            at = slice(b * block, (b + 1) * block)
+            apart = jnp.dot(held[at, n * wide : (n + 1) * wide], split, preferred_element_type=jnp.float32)
+            apart = apart.astype(jnp.bfloat16)
+            halves[0, at, n * LANES : (n + 1) * LANES] = apart[:, :LANES]
+            halves[1, at, n * LANES : (n + 1) * LANES] = apart[:, LANES:]
 
     def index_copy(k, slot):
         number, device = other(k, place)[2:]
@@ -150,29 +171,35 @@
         index_copy(k, me).start()
         return carry
 
-    lax.fori_loop(1, CHIPS, send_index, 0)
-    for load in loads:
-        load.wait()
-
     def chunk_step(t, carry):
-        chunk = lax.rem(t + me, 8)
-        fill_table(table, rows_ref, turns_ref, chunk // 4, chunk)
-        total = None
+        q = lax.rem(t + me, 4)
+        fill_tables(table, rows_ref, turns_ref, q)
+        first = (lax.broadcasted_iota(jnp.int32, (1, LANES), 1) + q) == 0
+        sums = [None, None]
         for b in range(slots // block):
-            both = jnp.dot(held[b * block : (b + 1) * block], table[...], preferred_element_type=jnp.float32)
-            real, imag = both[:, :LANES], both[:, LANES:]
-            logs = jnp.log((real * real + imag * imag) * (1.0 / samples) + 1e-6)
-            part = jnp.dot(
-                hot[:, b * block : (b + 1) * block], two_parts(logs, 1), preferred_element_type=jnp.float32
-            )
-            total = part if total is None else total + part
-        total = (total[:, :LANES] + total[:, LANES:]).T
-        at = pl.ds(chunk * 8, 8)
-        blocks[at, :OWNED, :] = total[:, :LANES].reshape(8, OWNED, LANES)
-        blocks[at, OWNED:, :] = total[:, LANES:].reshape(8, OWNED, LANES)
+            at = slice(b * block, (b + 1) * block)
+            even = jnp.dot(halves[0, at], table[0], preferred_element_type=jnp.float32)
+            odd = jnp.dot(halves[1, at], table[1], preferred_element_type=jnp.float32)
+            even_c, even_s, odd_c, odd_s = even[:, :LANES], even[:, LANES:], odd[:, :LANES], odd[:, LANES:]
+            whole = (even_c + odd_c, jnp.where(first, 0.0, even_s + odd_s))
+            mirror = (jnp.where(first, even_s, even_c - odd_c), jnp.where(first, odd_s, even_s - odd_s))
+            for n, (real, imag) in enumerate((whole, mirror)):
+                logs = jnp.log((real * real + imag * imag) * (1.0 / samples) + 1e-6)
+                part = jnp.dot(hot[:, at], two_parts(logs, 1), preferred_element_type=jnp.float32)
+                sums[n] = part if b == 0 else sums[n] + part
+        for n in range(2):
+            total = (sums[n][:, :LANES] + sums[n][:, LANES:]).T
+            at = pl.ds(q * 16 + n * 8, 8)
+            blocks[at, :OWNED, :] = total[:, :LANES].reshape(8, OWNED, LANES)
+            blocks[at, OWNED:, :] = total[:, LANES:].reshape(8, OWNED, LANES)
+
+        @pl.when(t == 0)
+        def _():
+            all_here()
+            lax.fori_loop(1, CHIPS, send_index, 0)
 
         def send(n, inner):
-            number = chunk * 8 + n
+            number = q * 16 + n
 
             @pl.when(number != me)
             def _():
@@ -180,34 +207,35 @@
 
             return inner
 
-        lax.fori_loop(0, 8, send, 0)
-        return carry
-
-    lax.fori_loop(0, 8, chunk_step, 0)
+        lax.fori_loop(0, 16, send, 0)
+        return carry
+
+    lax.fori_loop(0, 4, chunk_step, 0)
     landed[me] = blocks[me]
 
     totals[...] = jnp.zeros_like(totals)
-    rcv_count[...] = jnp.zeros_like(rcv_count)
-
-    def pair_step(number):
-        ty, j = number // PLANE, lax.rem(number, PLANE)
-        values = index_landed[number].astype(jnp.float32)
-        shots = jnp.concatenate([one_hot(values[r : r + 1], ids) for r in range(tiles)], axis=1)
-        rcvs = jnp.concatenate([one_hot(values[tiles + r : tiles + r + 1], ids) for r in range(tiles)], axis=1)
-        pair = lax.dot_general(shots, rcvs, NT, preferred_element_type=jnp.float32)
+
+    def index_wait(k, carry):
+        index_copy(k, None).wait()
+        return carry
+
+    lax.fori_loop(1, CHIPS, index_wait, 0)
+
+    def pair_step(j, carry):
         across = pl.ds(pl.multiple_of(j * LANES, LANES), LANES)
-        pairs[pl.ds(pl.multiple_of(ty * LANES, LANES), LANES), across] = pair.astype(jnp.bfloat16)
-        totals[ty] += pair
-        rcv_count[:, across] += jnp.broadcast_to(pair.sum(axis=0, keepdims=True), (8, LANES))
-
-    pair_step(me)
-
-    def pair_loop(k, carry):
-        index_copy(k, None).wait()
-        pair_step(other(k, place)[2])
-        return carry
-
-    lax.fori_loop(1, CHIPS, pair_loop, 0)
+        count = None
+        for b in range(RINGS):
+            values = index_landed[b * PLANE + j].astype(jnp.float32)
+            shots = jnp.concatenate([one_hot(values[r : r + 1], ids) for r in range(tiles)], axis=1)
+            rcvs = jnp.concatenate([one_hot(values[tiles + r : tiles + r + 1], ids) for r in range(tiles)], axis=1)
+            pair = lax.dot_general(shots, rcvs, NT, preferred_element_type=jnp.float32)
+            pairs[b * LANES : (b + 1) * LANES, across] = pair.astype(jnp.bfloat16)
+            totals[b] += pair
+            count = pair if count is None else count + pair
+        rcv_count[:, across] = jnp.broadcast_to(count.sum(axis=0, keepdims=True), (8, LANES))
+        return carry
+
+    lax.fori_loop(0, PLANE, pair_step, 0, unroll=2)
 
     def pair_copy(src, dst, n):
         return pltpu.make_async_remote_copy(
@@ -284,12 +312,18 @@
     rcv_out[...] = rcv_land[...]
 
 
-def turn_kernel(shot_in, rcv_in, shot_out, rcv_out, order):
-    half = order.shape[0] // 2
+def turn_kernel(shot_in, rcv_in, shot_out, rcv_out):
+    lane = lax.broadcasted_iota(jnp.int32, (LANES, LANES), 1)
+    back = lax.rem(LANES - lane, LANES)
     for src, dst in ((shot_in, shot_out), (rcv_in, rcv_out)):
-        order[pl.ds(0, half, stride=2), :] = src[:half]
-        order[pl.ds(1, half, stride=2), :] = src[half:]
-        dst[...] = order[...].T
+        mirrors = []
+        for q in range(4):
+            at = 2 * q * LANES
+            dst[:, q * LANES : (q + 1) * LANES] = src[at : at + LANES].T
+            mirrors.append(jnp.take_along_axis(src[at + LANES : at + 2 * LANES].T, back, axis=1))
+        for c in range(4, 8):
+            head = mirrors[8 - c if c > 4 else 0]
+            dst[:, c * LANES : (c + 1) * LANES] = jnp.where(lane == 0, head, mirrors[7 - c])
 
 
 def shards(traces, trace_shot, trace_rcv, fold_count):
@@ -297,20 +331,19 @@
     bins = samples // 2
     tiles = slots // LANES
     rows_np, turns_np = phase_tables(samples)
-    alive = jnp.arange(slots, dtype=jnp.int32).reshape(1, tiles, LANES) < fold_count[0, 0]
-    index = jnp.stack([trace_shot[0, 0], trace_rcv[0, 0]]).reshape(2, tiles, LANES)
-    index = jnp.where(alive, index, -1).reshape(2 * tiles, LANES)
     f32, bf16 = jnp.float32, jnp.bfloat16
     vmem = pl.BlockSpec(memory_space=VMEM)
     shape = jax.ShapeDtypeStruct
     shot_got, rcv_got = pl.pallas_call(
         main_kernel,
         out_shape=(shape((CHIPS, OWNED, LANES), f32), shape((CHIPS, OWNED, LANES), f32)),
-        in_specs=[pl.BlockSpec(memory_space=pl.ANY), vmem, vmem, vmem],
+        in_specs=[pl.BlockSpec(memory_space=pltpu.SMEM), vmem, vmem, pl.BlockSpec(memory_space=pl.ANY), vmem, vmem],
         out_specs=(vmem,) * 2,
         scratch_shapes=[
+            VMEM((2 * tiles, LANES), jnp.int32),
             VMEM((slots, samples), bf16),
-            VMEM((samples, 2 * LANES), bf16),
+            VMEM((2, slots, samples // 2), bf16),
+            VMEM((2, samples // 2, 2 * LANES), bf16),
             VMEM((2 * LANES, slots), bf16),
             VMEM((CHIPS, 2 * OWNED, LANES), f32),
             VMEM((CHIPS, 2 * OWNED, LANES), f32),
@@ -334,13 +367,12 @@
             collective_id=0, has_side_effects=True, vmem_limit_bytes=VMEM_LIMIT
         ),
         name="decompose",
-    )(traces[0, 0], index, jnp.asarray(rows_np), jnp.asarray(turns_np))
+    )(fold_count, trace_shot[0], trace_rcv[0], traces[0, 0], jnp.asarray(rows_np), jnp.asarray(turns_np))
     return pl.pallas_call(
         turn_kernel,
         out_shape=(shape((LANES, bins), f32), shape((LANES, bins), f32)),
         in_specs=[vmem] * 2,
         out_specs=(vmem,) * 2,
-        scratch_shapes=[VMEM((bins, LANES), f32)],
         compiler_params=pltpu.CompilerParams(vmem_limit_bytes=VMEM_LIMIT),
         name="turn",
     )(shot_got.reshape(bins, LANES), rcv_got.reshape(bins, LANES))

time: 86.1 us -> 72.9 us (0.85)
  Pallas kernels: 82.3 us -> 70.6 us
  other arithmetic: 1.45 us -> 0 us
    pallas_call x1, Pallas kernels: 79.9 us -> 68 us  [shards(): pl.pallas_call(main_kernel, out_shape=(shape((CHIPS, OWNED, LANES), f32),...]
    unnamed x2 -> x0, other arithmetic: 1.43 us -> none
where the time goes in v3:
time: 72.9 us; the launch traced here: 71.9 us
  Pallas kernels  70.6 us (97%)
  between operations  1.29 us (2%)
    pallas_call x1, Pallas kernels, shards(): pl.pallas_call(main_kernel, out_shape=(shape((CHIPS, OWNED, LANES), f32),...  68 us
    pallas_call x1, Pallas kernels, shards(): pl.pallas_call(turn_kernel, out_shape=(shape((LANES, bins), f32), shape((...  2.59 us

profile of v3, /device:TPU:1, one launch (start us, length us, event | category | flops | bytes accessed | tf_op | source)
XLA Modules:
  0.0 71.9 jit_solution(9731840100205048530)
XLA Ops:
  1.3 68.0 %decompose.1 = (f32[64,16,128]{2,1,0:T(8,128)}, f32[64,16,128]{2,1,0:T(8,128)}) custom-call(s32[1,1]{1,0:T(1,128)S(6)} %copy.8.fold, s32[1,1536]{1,0:T(1,128)} %bitcast.8, s32[1,1536]{1,0:T(1,128)} %bitcast.9, bf16[1536,2048]{1,0:T(8,128)(2,1)} %bitcast.5, f32[2,128,128]{2,1,0:T(8,128)} %constant.4.clone.rows_ref, f32[4,2,2,8,128]{4,3,2,1,0:T(8,128)} %constant.5.clone.turns_ref), custom_call_target="tpu_custom_call" | custom-call | tf_op jit(solution)/shard_map/decompose/pallas_call | solution.py:337
  69.3 2.6 %turn.1 = (f32[128,1024]{1,0:T(8,128)}, f32[128,1024]{1,0:T(8,128)}) custom-call(f32[1024,128]{1,0:T(8,128)} %bitcast.6, f32[1024,128]{1,0:T(8,128)} %bitcast.7), custom_call_target="tpu_custom_call" | custom-call | tf_op jit(solution)/shard_map/turn/pallas_call | solution.py:371

commit v4 on v3

--- a/solution.py
+++ b/solution.py
@@ -77,29 +77,14 @@
     return shot // 2, lax.rem(shot, 2), rcv // 4, lax.rem(rcv, 4)
 
 
-def other(k, place):
+def others(place):
     y, core, z, x = place
-    ty = lax.rem(y + k // 16, 4)
-    tz = lax.rem(z + lax.rem(k // 4, 4), 4)
-    tx = lax.rem(x + lax.rem(k, 4), 4)
-    rcv = tz * 4 + tx
-    return ty, rcv, ty * PLANE + rcv, (ty * 2 + core, rcv)
-
-
-def device_of(number, core):
-    return (number // PLANE) * 2 + core, lax.rem(number, PLANE)
-
-
-def greet(place, partner):
-    barrier = pltpu.get_barrier_semaphore()
-
-    def step(k, carry):
-        pl.semaphore_signal(barrier, inc=1, device_id=other(k, place)[3], device_id_type=MESH)
-        return carry
-
-    lax.fori_loop(1, CHIPS, step, 0)
-    pl.semaphore_signal(barrier, inc=1, device_id=partner, device_id_type=MESH)
-    return lambda: pl.semaphore_wait(barrier, CHIPS)
+    ys, zs, xs = ([lax.rem(at + d, RINGS) for d in range(RINGS)] for at in (y, z, x))
+    found = []
+    for k in range(1, CHIPS):
+        ty, rcv = ys[k // PLANE], zs[k // 4 % 4] * 4 + xs[k % 4]
+        found.append((ty, rcv, ty * PLANE + rcv, (ty * 2 + core, rcv)))
+    return found
 
 
 def two_parts(value, axis):
@@ -108,10 +93,11 @@
 
 
 def main_kernel(fold, trace_shot, trace_rcv, traces, rows_ref, turns_ref, shot_out, rcv_out,
-                index, held, halves, table, hot, blocks, landed, index_landed,
+                index, held, halves, table, hot, shot_blocks, rcv_blocks, pre_send, pre_land,
+                shot_landed, rcv_landed, index_landed,
                 pairs, totals, rcv_count, count_land,
                 shot_send, rcv_send, shot_land, rcv_land, part_send, part_land,
-                trace_sem, sems, term_sems, part_sems):
+                trace_sem, sems, pre_sems, part_sems):
     place = my_place()
     y, core, z, x = place
     mine = z * 4 + x
@@ -119,8 +105,21 @@
     partner = (y * 2 + 1 - core, mine)
     slots, samples = held.shape
     tiles = slots // LANES
-
-    all_here = greet(place, partner)
+    away = others(place)
+
+    barrier = pltpu.get_barrier_semaphore()
+    for device in [a[3] for a in away] + [partner]:
+        pl.semaphore_signal(barrier, inc=1, device_id=device, device_id_type=MESH)
+
+    def send(src, dst, kind, device):
+        pltpu.make_async_remote_copy(
+            src, dst, sems.at[0, kind], sems.at[1, kind], device_id=device, device_id_type=MESH
+        ).start()
+
+    def settle(ref, kind, way):
+        span = ref.at[pl.ds(0, CHIPS - 1)]
+        pltpu.make_async_copy(span, span, sems.at[way, kind]).wait()
+
     block = 512
     loads = [
         pltpu.make_async_copy(traces.at[pl.ds(b * block, block)], held.at[pl.ds(b * block, block)], trace_sem.at[b])
@@ -154,22 +153,22 @@
             halves[0, at, n * LANES : (n + 1) * LANES] = apart[:, :LANES]
             halves[1, at, n * LANES : (n + 1) * LANES] = apart[:, LANES:]
 
-    def index_copy(k, slot):
-        number, device = other(k, place)[2:]
+    def pre_copy(t):
         return pltpu.make_async_remote_copy(
-            index, index_landed.at[number if slot is None else slot], sems.at[0, number],
-            sems.at[1, number if slot is None else slot], device_id=device, device_id_type=MESH
+            pre_send.at[t], pre_land.at[t], pre_sems.at[0, t], pre_sems.at[1, t],
+            device_id=partner, device_id_type=MESH
         )
 
-    def block_copy(number, slot):
-        return pltpu.make_async_remote_copy(
-            blocks.at[number], landed.at[slot], sems.at[2, number], sems.at[3, slot],
-            device_id=device_of(number, core), device_id_type=MESH
-        )
-
-    def send_index(k, carry):
-        index_copy(k, me).start()
-        return carry
+    def send_rcv(t):
+        q = lax.rem(t + me, RINGS)
+        pre_copy(t).wait()
+        at = pl.ds(q * PLANE, PLANE)
+        rcv_blocks[at] = rcv_blocks[at] + pre_land[t]
+        for n in range(PLANE):
+
+            @pl.when(q * PLANE + n != me)
+            def _():
+                send(rcv_blocks.at[q * PLANE + n], rcv_landed.at[me], 2, (q * 2 + core, n))
 
     def chunk_step(t, carry):
         q = lax.rem(t + me, 4)
@@ -189,37 +188,36 @@
                 sums[n] = part if b == 0 else sums[n] + part
         for n in range(2):
             total = (sums[n][:, :LANES] + sums[n][:, LANES:]).T
-            at = pl.ds(q * 16 + n * 8, 8)
-            blocks[at, :OWNED, :] = total[:, :LANES].reshape(8, OWNED, LANES)
-            blocks[at, OWNED:, :] = total[:, LANES:].reshape(8, OWNED, LANES)
+            shot_blocks[pl.ds(q * PLANE + n * 8, 8)] = total[:, :LANES].reshape(8, OWNED, LANES)
+            both = total[:, LANES:].reshape(8, 2, OWNED // 2, LANES)
+            rcv_blocks[pl.ds(q * PLANE + n * 8, 8)] = jnp.where(core == 0, both[:, 0], both[:, 1])
+            pre_send[t, n * 8 : n * 8 + 8] = jnp.where(core == 0, both[:, 1], both[:, 0])
 
         @pl.when(t == 0)
         def _():
-            all_here()
-            lax.fori_loop(1, CHIPS, send_index, 0)
-
-        def send(n, inner):
-            number = q * 16 + n
-
-            @pl.when(number != me)
+            pl.semaphore_wait(barrier, CHIPS)
+            for _, _, _, device in away:
+                send(index, index_landed.at[me], 0, device)
+
+        pre_copy(t).start()
+        for n in range(PLANE):
+
+            @pl.when(q * PLANE + n != me)
             def _():
-                block_copy(number, me).start()
-
-            return inner
-
-        lax.fori_loop(0, 16, send, 0)
+                send(shot_blocks.at[q * PLANE + n], shot_landed.at[me], 1, (q * 2 + core, n))
+
+        @pl.when(t > 0)
+        def _():
+            send_rcv(t - 1)
+
         return carry
 
-    lax.fori_loop(0, 4, chunk_step, 0)
-    landed[me] = blocks[me]
+    lax.fori_loop(0, RINGS, chunk_step, 0)
+    shot_landed[me] = shot_blocks[me]
 
     totals[...] = jnp.zeros_like(totals)
 
-    def index_wait(k, carry):
-        index_copy(k, None).wait()
-        return carry
-
-    lax.fori_loop(1, CHIPS, index_wait, 0)
+    settle(index_landed, 0, 1)
 
     def pair_step(j, carry):
         across = pl.ds(pl.multiple_of(j * LANES, LANES), LANES)
@@ -235,7 +233,10 @@
         rcv_count[:, across] = jnp.broadcast_to(count.sum(axis=0, keepdims=True), (8, LANES))
         return carry
 
-    lax.fori_loop(0, PLANE, pair_step, 0, unroll=2)
+    lax.fori_loop(0, 4, pair_step, 0, unroll=2)
+    send_rcv(RINGS - 1)
+    rcv_landed[me] = rcv_blocks[me]
+    lax.fori_loop(4, PLANE, pair_step, 0, unroll=2)
 
     def pair_copy(src, dst, n):
         return pltpu.make_async_remote_copy(
@@ -246,38 +247,21 @@
     count_copy.start()
     counts = jnp.concatenate([totals[b].T.sum(axis=0, keepdims=True) for b in range(RINGS)], axis=1)
 
-    def block_wait(k, carry):
-        number = other(k, place)[2]
-        block_copy(number, number).wait()
-        return carry
-
-    lax.fori_loop(1, CHIPS, block_wait, 0)
+    settle(shot_landed, 1, 1)
+    settle(rcv_landed, 2, 1)
     shot_logs = jnp.concatenate(
-        [landed[b * PLANE : (b + 1) * PLANE, :OWNED, :].sum(axis=0) for b in range(RINGS)], axis=1
+        [shot_landed[b * PLANE : (b + 1) * PLANE].sum(axis=0) for b in range(RINGS)], axis=1
     )
-    rcv_logs = landed[:PLANE, OWNED:, :]
+    rcv_logs = rcv_landed[:PLANE]
     for b in range(1, RINGS):
-        rcv_logs = rcv_logs + landed[b * PLANE : (b + 1) * PLANE, OWNED:, :]
+        rcv_logs = rcv_logs + rcv_landed[b * PLANE : (b + 1) * PLANE]
     rcv_logs = jnp.concatenate([rcv_logs[j] for j in range(PLANE)], axis=1)
+    rcv_logs = jnp.concatenate(
+        [jnp.where(core == 0, rcv_logs, 0.0), jnp.where(core == 0, 0.0, rcv_logs)], axis=0
+    )
     count_copy.wait()
     rcv_counts = rcv_count[0:1, :] + count_land[0:1, :]
     copies = [pair_copy(part_send.at[n], part_land.at[n], n) for n in range(SWEEPS)]
-
-    def copy_to(src, dst, kind, k, sending):
-        ty, rcv, number, device = other(k, place)
-        at = me if sending else number
-        source = src.at[ty] if kind == 0 else src.at[rcv]
-        return pltpu.make_async_remote_copy(
-            source, dst.at[at], term_sems.at[2 * kind, number], term_sems.at[2 * kind + 1, at],
-            device_id=device, device_id_type=MESH
-        )
-
-    def send_all(src, dst, kind):
-        def step(k, carry):
-            copy_to(src, dst, kind, k, True).start()
-            return carry
-
-        lax.fori_loop(1, CHIPS, step, 0)
 
     rcv_terms = None
     for n in range(SWEEPS):
@@ -289,38 +273,47 @@
         if n == SWEEPS - 1:
             for b in range(RINGS):
                 shot_send[b] = shot_terms[:, b * LANES : (b + 1) * LANES]
-            send_all(shot_send, shot_land, 0)
+            for ty, _, _, device in away:
+                send(shot_send.at[ty], shot_land.at[me], 3, device)
         both = jnp.dot(two_parts(shot_terms, 0), pairs[...], preferred_element_type=jnp.float32)
         part = rcv_logs - (both[:OWNED] + both[OWNED:])
         part_send[n] = part
         copies[n].start()
         copies[n].wait()
         rcv_terms = (part + part_land[n]) / rcv_counts
+    own = jnp.where(core == 0, rcv_terms[: OWNED // 2], rcv_terms[OWNED // 2 :])
     for j in range(PLANE):
-        rcv_send[j] = rcv_terms[:, j * LANES : (j + 1) * LANES]
-    send_all(rcv_send, rcv_land, 1)
+        rcv_send[j] = own[:, j * LANES : (j + 1) * LANES]
+    for _, rcv, _, device in away:
+        send(rcv_send.at[rcv], rcv_land.at[core, me], 4, device)
     shot_land[me] = shot_send[y]
-    rcv_land[me] = rcv_send[mine]
-
-    def finish(k, carry):
-        copy_to(shot_send, shot_land, 0, k, False).wait()
-        copy_to(rcv_send, rcv_land, 1, k, False).wait()
-        return carry
-
-    lax.fori_loop(1, CHIPS, finish, 0)
+    rcv_land[core, me] = rcv_send[mine]
+    settle(rcv_land.at[core], 4, 1)
+    across = pair_copy(rcv_land.at[core], rcv_land.at[core], SWEEPS + 1)
+    across.start()
+    settle(shot_land, 3, 1)
     shot_out[...] = shot_land[...]
+    for kind, ref in enumerate((index_landed, shot_landed, rcv_landed, shot_land, rcv_landed)):
+        settle(ref, kind, 0)
+    across.wait()
     rcv_out[...] = rcv_land[...]
 
 
 def turn_kernel(shot_in, rcv_in, shot_out, rcv_out):
     lane = lax.broadcasted_iota(jnp.int32, (LANES, LANES), 1)
     back = lax.rem(LANES - lane, LANES)
+    def chunk(src, n):
+        if src.shape[0] == CHIPS:
+            bins = src[n * 8 : n * 8 + 8]
+        else:
+            bins = jnp.stack([src[0, n * 8 : n * 8 + 8], src[1, n * 8 : n * 8 + 8]], axis=1)
+        return bins.reshape(LANES, LANES).T
+
     for src, dst in ((shot_in, shot_out), (rcv_in, rcv_out)):
         mirrors = []
         for q in range(4):
-            at = 2 * q * LANES
-            dst[:, q * LANES : (q + 1) * LANES] = src[at : at + LANES].T
-            mirrors.append(jnp.take_along_axis(src[at + LANES : at + 2 * LANES].T, back, axis=1))
+            dst[:, q * LANES : (q + 1) * LANES] = chunk(src, 2 * q)
+            mirrors.append(jnp.take_along_axis(chunk(src, 2 * q + 1), back, axis=1))
         for c in range(4, 8):
             head = mirrors[8 - c if c > 4 else 0]
             dst[:, c * LANES : (c + 1) * LANES] = jnp.where(lane == 0, head, mirrors[7 - c])
@@ -336,7 +329,7 @@
     shape = jax.ShapeDtypeStruct
     shot_got, rcv_got = pl.pallas_call(
         main_kernel,
-        out_shape=(shape((CHIPS, OWNED, LANES), f32), shape((CHIPS, OWNED, LANES), f32)),
+        out_shape=(shape((CHIPS, OWNED, LANES), f32), shape((2, CHIPS, OWNED // 2, LANES), f32)),
         in_specs=[pl.BlockSpec(memory_space=pltpu.SMEM), vmem, vmem, pl.BlockSpec(memory_space=pl.ANY), vmem, vmem],
         out_specs=(vmem,) * 2,
         scratch_shapes=[
@@ -345,23 +338,27 @@
             VMEM((2, slots, samples // 2), bf16),
             VMEM((2, samples // 2, 2 * LANES), bf16),
             VMEM((2 * LANES, slots), bf16),
-            VMEM((CHIPS, 2 * OWNED, LANES), f32),
-            VMEM((CHIPS, 2 * OWNED, LANES), f32),
+            VMEM((CHIPS, OWNED, LANES), f32),
+            VMEM((CHIPS, OWNED // 2, LANES), f32),
+            VMEM((RINGS, PLANE, OWNED // 2, LANES), f32),
+            VMEM((RINGS, PLANE, OWNED // 2, LANES), f32),
+            VMEM((CHIPS, OWNED, LANES), f32),
+            VMEM((CHIPS, OWNED // 2, LANES), f32),
             VMEM((CHIPS, 2 * tiles, LANES), jnp.int32),
             VMEM((RINGS * LANES, PLANE * LANES), bf16),
             VMEM((RINGS, LANES, LANES), f32),
             VMEM((8, PLANE * LANES), f32),
             VMEM((8, PLANE * LANES), f32),
             VMEM((RINGS, OWNED, LANES), f32),
-            VMEM((PLANE, OWNED, LANES), f32),
+            VMEM((PLANE, OWNED // 2, LANES), f32),
             VMEM((CHIPS, OWNED, LANES), f32),
-            VMEM((CHIPS, OWNED, LANES), f32),
+            VMEM((2, CHIPS, OWNED // 2, LANES), f32),
             VMEM((SWEEPS, OWNED, PLANE * LANES), f32),
             VMEM((SWEEPS, OWNED, PLANE * LANES), f32),
             pltpu.SemaphoreType.DMA((slots // 512,)),
-            pltpu.SemaphoreType.DMA((4, CHIPS)),
-            pltpu.SemaphoreType.DMA((4, CHIPS)),
-            pltpu.SemaphoreType.DMA((2, SWEEPS + 1)),
+            pltpu.SemaphoreType.DMA((2, 5)),
+            pltpu.SemaphoreType.DMA((2, RINGS)),
+            pltpu.SemaphoreType.DMA((2, SWEEPS + 2)),
         ],
         compiler_params=pltpu.CompilerParams(
             collective_id=0, has_side_effects=True, vmem_limit_bytes=VMEM_LIMIT
@@ -375,7 +372,7 @@
         out_specs=(vmem,) * 2,
         compiler_params=pltpu.CompilerParams(vmem_limit_bytes=VMEM_LIMIT),
         name="turn",
-    )(shot_got.reshape(bins, LANES), rcv_got.reshape(bins, LANES))
+    )(shot_got, rcv_got)
 
 
 def solution(mesh):

time: 72.9 us -> 63 us (0.86); the launches traced: 71.9 us -> 62.8 us
  Pallas kernels: 70.6 us -> 61.5 us
    pallas_call x1, Pallas kernels: 68 us -> 58.9 us  [shards(): pl.pallas_call(main_kernel, out_shape=(shape((CHIPS, OWNED, LANES), f32),...]
where the time goes in v4:
time: 63 us; the launch traced here: 62.8 us
  Pallas kernels  61.5 us (98%)
  between operations  1.29 us (2%)
    pallas_call x1, Pallas kernels, shards(): pl.pallas_call(main_kernel, out_shape=(shape((CHIPS, OWNED, LANES), f32),...  58.9 us
    pallas_call x1, Pallas kernels, shards(): pl.pallas_call(turn_kernel, out_shape=(shape((LANES, bins), f32), shape((...  2.59 us

profile of v4, /device:TPU:1, one launch (start us, length us, event | category | flops | bytes accessed | tf_op | source)
XLA Modules:
  0.0 62.8 jit_solution(3915744427678870592)
XLA Ops:
  1.3 58.9 %decompose.1 = (f32[64,16,128]{2,1,0:T(8,128)}, f32[2,64,8,128]{3,2,1,0:T(8,128)}) custom-call(s32[1,1]{1,0:T(1,128)S(6)} %copy.8.fold, s32[1,1536]{1,0:T(1,128)} %bitcast.4, s32[1,1536]{1,0:T(1,128)} %bitcast.5, bf16[1536,2048]{1,0:T(8,128)(2,1)} %bitcast.3, f32[2,128,128]{2,1,0:T(8,128)} %constant.4.clone.rows_ref, ...), custom_call_target="tpu_custom_call" | custom-call | tf_op jit(solution)/shard_map/decompose/pallas_call | solution.py:330
  60.2 2.6 %turn.1 = (f32[128,1024]{1,0:T(8,128)}, f32[128,1024]{1,0:T(8,128)}) custom-call(f32[64,16,128]{2,1,0:T(8,128)} %get-tuple-element.4.shot_in, f32[2,64,8,128]{3,2,1,0:T(8,128)} %get-tuple-element.5.rcv_in), custom_call_target="tpu_custom_call" | custom-call | tf_op jit(solution)/shard_map/turn/pallas_call | solution.py:368

commit v5 on v4

--- a/solution.py
+++ b/solution.py
@@ -97,7 +97,7 @@
                 shot_landed, rcv_landed, index_landed,
                 pairs, totals, rcv_count, count_land,
                 shot_send, rcv_send, shot_land, rcv_land, part_send, part_land,
-                trace_sem, sems, pre_sems, part_sems):
+                trace_sem, index_sems, sems, pre_sems, part_sems):
     place = my_place()
     y, core, z, x = place
     mine = z * 4 + x
@@ -138,7 +138,8 @@
     for r in range(tiles):
         hot[:LANES, r * LANES : (r + 1) * LANES] = one_hot(values[r : r + 1], ids)
         hot[LANES:, r * LANES : (r + 1) * LANES] = one_hot(values[tiles + r : tiles + r + 1], ids)
-    index_landed[me] = index[...]
+    for part in range(3):
+        index_landed[part, y, z, x] = index[8 * part : 8 * part + 8, :]
     wide = 2 * LANES
     rank = lax.broadcasted_iota(jnp.int32, (wide, wide), 0)
     spot = lax.broadcasted_iota(jnp.int32, (wide, wide), 1)
@@ -153,6 +154,26 @@
             halves[0, at, n * LANES : (n + 1) * LANES] = apart[:, :LANES]
             halves[1, at, n * LANES : (n + 1) * LANES] = apart[:, LANES:]
 
+    def index_step(stage):
+        for part in range(3):
+            order = [(2, 1, 0), (1, 0, 2), (0, 2, 1)][part]
+            at = [y, z, x]
+            for ring in order[:stage]:
+                at[ring] = slice(None)
+            ref = index_landed.at[(part, *at)]
+            for d in range(1, RINGS):
+                to = [y, z, x]
+                to[order[stage]] = lax.rem(to[order[stage]] + d, RINGS)
+                pltpu.make_async_remote_copy(
+                    ref, ref, index_sems.at[0, part, stage], index_sems.at[1, part, stage],
+                    device_id=(to[0] * 2 + core, to[1] * 4 + to[2]), device_id_type=MESH
+                ).start()
+
+    def index_settle(stage, way):
+        for part in range(3):
+            span = index_landed.at[(part,) + (0,) * (2 - stage) + (pl.ds(0, 3),)]
+            pltpu.make_async_copy(span, span, index_sems.at[way, part, stage]).wait()
+
     def pre_copy(t):
         return pltpu.make_async_remote_copy(
             pre_send.at[t], pre_land.at[t], pre_sems.at[0, t], pre_sems.at[1, t],
@@ -169,6 +190,9 @@
             @pl.when(q * PLANE + n != me)
             def _():
                 send(rcv_blocks.at[q * PLANE + n], rcv_landed.at[me], 2, (q * 2 + core, n))
+
+    pl.semaphore_wait(barrier, CHIPS)
+    index_step(0)
 
     def chunk_step(t, carry):
         q = lax.rem(t + me, 4)
@@ -195,9 +219,14 @@
 
         @pl.when(t == 0)
         def _():
-            pl.semaphore_wait(barrier, CHIPS)
-            for _, _, _, device in away:
-                send(index, index_landed.at[me], 0, device)
+            pass
+
+        for stage in range(1, 3):
+
+            @pl.when(t == stage - 1)
+            def _():
+                index_settle(stage - 1, 1)
+                index_step(stage)
 
         pre_copy(t).start()
         for n in range(PLANE):
@@ -217,13 +246,14 @@
 
     totals[...] = jnp.zeros_like(totals)
 
-    settle(index_landed, 0, 1)
+    index_settle(2, 1)
 
     def pair_step(j, carry):
         across = pl.ds(pl.multiple_of(j * LANES, LANES), LANES)
         count = None
         for b in range(RINGS):
-            values = index_landed[b * PLANE + j].astype(jnp.float32)
+            values = jnp.concatenate([index_landed[part, b, j // 4, lax.rem(j, 4)] for part in range(3)], axis=0)
+            values = values.astype(jnp.float32)
             shots = jnp.concatenate([one_hot(values[r : r + 1], ids) for r in range(tiles)], axis=1)
             rcvs = jnp.concatenate([one_hot(values[tiles + r : tiles + r + 1], ids) for r in range(tiles)], axis=1)
             pair = lax.dot_general(shots, rcvs, NT, preferred_element_type=jnp.float32)
@@ -293,8 +323,10 @@
     across.start()
     settle(shot_land, 3, 1)
     shot_out[...] = shot_land[...]
-    for kind, ref in enumerate((index_landed, shot_landed, rcv_landed, shot_land, rcv_landed)):
-        settle(ref, kind, 0)
+    for kind, ref in enumerate((shot_landed, rcv_landed, shot_land, rcv_landed)):
+        settle(ref, kind + 1, 0)
+    for stage in range(3):
+        index_settle(stage, 0)
     across.wait()
     rcv_out[...] = rcv_land[...]
 
@@ -344,7 +376,7 @@
             VMEM((RINGS, PLANE, OWNED // 2, LANES), f32),
             VMEM((CHIPS, OWNED, LANES), f32),
             VMEM((CHIPS, OWNED // 2, LANES), f32),
-            VMEM((CHIPS, 2 * tiles, LANES), jnp.int32),
+            VMEM((3, RINGS, RINGS, RINGS, 8, LANES), jnp.int32),
             VMEM((RINGS * LANES, PLANE * LANES), bf16),
             VMEM((RINGS, LANES, LANES), f32),
             VMEM((8, PLANE * LANES), f32),
@@ -356,6 +388,7 @@
             VMEM((SWEEPS, OWNED, PLANE * LANES), f32),
             VMEM((SWEEPS, OWNED, PLANE * LANES), f32),
             pltpu.SemaphoreType.DMA((slots // 512,)),
+            pltpu.SemaphoreType.DMA((2, 3, 3)),
             pltpu.SemaphoreType.DMA((2, 5)),
             pltpu.SemaphoreType.DMA((2, RINGS)),
             pltpu.SemaphoreType.DMA((2, SWEEPS + 2)),

time: 63 us -> 59 us (0.937)
  Pallas kernels: 61.5 us -> 57.6 us
    pallas_call x1, Pallas kernels: 58.9 us -> 55 us  [shards(): pl.pallas_call(main_kernel, out_shape=(shape((CHIPS, OWNED, LANES), f32),...]
where the time goes in v5:
time: 59 us; the launch traced here: 58.9 us
  Pallas kernels  57.6 us (98%)
  between operations  1.29 us (2%)
    pallas_call x1, Pallas kernels, shards(): pl.pallas_call(main_kernel, out_shape=(shape((CHIPS, OWNED, LANES), f32),...  55 us
    pallas_call x1, Pallas kernels, shards(): pl.pallas_call(turn_kernel, out_shape=(shape((LANES, bins), f32), shape((...  2.59 us

profile of v5, /device:TPU:1, one launch (start us, length us, event | category | flops | bytes accessed | tf_op | source)
XLA Modules:
  0.0 58.9 jit_solution(11923741735369034343)
XLA Ops:
  1.3 55.0 %decompose.1 = (f32[64,16,128]{2,1,0:T(8,128)}, f32[2,64,8,128]{3,2,1,0:T(8,128)}) custom-call(s32[1,1]{1,0:T(1,128)S(6)} %copy.8.fold, s32[1,1536]{1,0:T(1,128)} %bitcast.4, s32[1,1536]{1,0:T(1,128)} %bitcast.5, bf16[1536,2048]{1,0:T(8,128)(2,1)} %bitcast.3, f32[2,128,128]{2,1,0:T(8,128)} %constant.4.clone.rows_ref, ...), custom_call_target="tpu_custom_call" | custom-call | tf_op jit(solution)/shard_map/decompose/pallas_call | solution.py:362
  56.3 2.6 %turn.1 = (f32[128,1024]{1,0:T(8,128)}, f32[128,1024]{1,0:T(8,128)}) custom-call(f32[64,16,128]{2,1,0:T(8,128)} %get-tuple-element.4.shot_in, f32[2,64,8,128]{3,2,1,0:T(8,128)} %get-tuple-element.5.rcv_in), custom_call_target="tpu_custom_call" | custom-call | tf_op jit(solution)/shard_map/turn/pallas_call | solution.py:401

commit v6 on v5

--- a/solution.py
+++ b/solution.py
@@ -1,6 +1,3 @@
-import functools
-import math
-
 import jax
 import jax.numpy as jnp
 import numpy as np
@@ -18,7 +15,7 @@
 RINGS = 4
 OWNED = 16
 NT = (((1,), (1,)), ((), ()))
-VMEM_LIMIT = 60 * 1024 * 1024
+VMEM_LIMIT = 50 * 1024 * 1024
 
 
 def phase_tables(samples):
@@ -303,7 +300,7 @@
         if n == SWEEPS - 1:
             for b in range(RINGS):
                 shot_send[b] = shot_terms[:, b * LANES : (b + 1) * LANES]
-            for ty, _, _, device in away:
+            for ty, _, _, device in away[::-1]:
                 send(shot_send.at[ty], shot_land.at[me], 3, device)
         both = jnp.dot(two_parts(shot_terms, 0), pairs[...], preferred_element_type=jnp.float32)
         part = rcv_logs - (both[:OWNED] + both[OWNED:])
@@ -314,7 +311,7 @@
     own = jnp.where(core == 0, rcv_terms[: OWNED // 2], rcv_terms[OWNED // 2 :])
     for j in range(PLANE):
         rcv_send[j] = own[:, j * LANES : (j + 1) * LANES]
-    for _, rcv, _, device in away:
+    for _, rcv, _, device in away[::-1]:
         send(rcv_send.at[rcv], rcv_land.at[core, me], 4, device)
     shot_land[me] = shot_send[y]
     rcv_land[core, me] = rcv_send[mine]
@@ -403,7 +400,7 @@
         out_shape=(shape((LANES, bins), f32), shape((LANES, bins), f32)),
         in_specs=[vmem] * 2,
         out_specs=(vmem,) * 2,
-        compiler_params=pltpu.CompilerParams(vmem_limit_bytes=VMEM_LIMIT),
+        compiler_params=pltpu.CompilerParams(vmem_limit_bytes=8 * 1024 * 1024),
         name="turn",
     )(shot_got, rcv_got)
 

time: 59 us -> 58.6 us (level)
  Pallas kernels: 57.6 us -> 54 us
  local copies, waits for them, and re-layouts: 0 us -> 3.12 us
    unnamed x0 -> x8, local copies, waits for them, and re-layouts: none -> 3.12 us
    pallas_call x1, Pallas kernels: 55 us -> 52.6 us  [shards(): pl.pallas_call(main_kernel, out_shape=(shape((CHIPS, OWNED, LANES), f32),...]
    pallas_call x1, Pallas kernels: 2.59 us -> 1.39 us  [shards(): pl.pallas_call(turn_kernel, out_shape=(shape((LANES, bins), f32), shape((...]
where the time goes in v6:
time: 58.6 us; the launch traced here: 58.4 us
  Pallas kernels  54 us (92%)
  local copies, waits for them, and re-layouts  3.12 us (5%)
  between operations  1.3 us (2%)
    pallas_call x1, Pallas kernels, shards(): pl.pallas_call(main_kernel, out_shape=(shape((CHIPS, OWNED, LANES), f32),...  52.6 us
    unnamed x8, local copies, waits for them, and re-layouts  3.12 us
    pallas_call x1, Pallas kernels, shards(): pl.pallas_call(turn_kernel, out_shape=(shape((LANES, bins), f32), shape((...  1.39 us

profile of v6, /device:TPU:1, one launch (start us, length us, event | category | flops | bytes accessed | tf_op | source)
XLA Modules:
  0.0 58.4 jit_solution(17292557454527182996)
XLA Ops:
  1.3 0.0 copy-start
  1.3 0.9 %copy-done = f32[2,128,128]{2,1,0:T(8,128)S(1)} copy-done((f32[2,128,128]{2,1,0:T(8,128)S(1)}, f32[2,128,128]{2,1,0:T(8,128)}, u32[]{:S(2)}) %copy-start) | copy-done | bytes 131096
  2.2 0.0 copy-start.1
  2.2 0.8 %copy-done.1 = f32[4,2,2,8,128]{4,3,2,1,0:T(8,128)S(1)} copy-done((f32[4,2,2,8,128]{4,3,2,1,0:T(8,128)S(1)}, f32[4,2,2,8,128]{4,3,2,1,0:T(8,128)}, u32[]{:S(2)}) %copy-start.1) | copy-done | bytes 65560
  3.0 0.0 copy-start.2
  3.0 0.7 %copy-done.2 = s32[1,1,1536]{2,1,0:T(1,128)S(1)} copy-done((s32[1,1,1536]{2,1,0:T(1,128)S(1)}, s32[1,1,1536]{2,1,0:T(1,128)}, u32[]{:S(2)}) %copy-start.2) | copy-done | bytes 6168
  3.7 0.0 copy-start.3
  3.7 0.7 %copy-done.3 = s32[1,1,1536]{2,1,0:T(1,128)S(1)} copy-done((s32[1,1,1536]{2,1,0:T(1,128)S(1)}, s32[1,1,1536]{2,1,0:T(1,128)}, u32[]{:S(2)}) %copy-start.3) | copy-done | bytes 6168
  4.4 52.6 %decompose.1 = (f32[64,16,128]{2,1,0:T(8,128)S(1)}, f32[2,64,8,128]{3,2,1,0:T(8,128)S(1)}) custom-call(s32[1,1]{1,0:T(1,128)S(6)} %copy.8.fold, s32[1,1536]{1,0:T(1,128)S(1)} %bitcast.3, s32[1,1536]{1,0:T(1,128)S(1)} %bitcast.4, bf16[1536,2048]{1,0:T(8,128)(2,1)} %bitcast.5, f32[2,128,128]{2,1,0:T(8,128)S(1)} %copy-done, f32[4,2,2,8,128]{4,3,2,1,0:T(8,128)S(1)} %copy-done.1), custom_call_target="tpu_custom_call" | custom-call | tf_op jit(solution)/shard_map/decompose/pallas_call | solution.py:359
  57.0 1.4 %turn.1 = (f32[128,1024]{1,0:T(8,128)}, f32[128,1024]{1,0:T(8,128)}) custom-call(f32[64,16,128]{2,1,0:T(8,128)S(1)} %get-tuple-element.4.shot_in, f32[2,64,8,128]{3,2,1,0:T(8,128)S(1)} %get-tuple-element.5.rcv_in), custom_call_target="tpu_custom_call" | custom-call | tf_op jit(solution)/shard_map/turn/pallas_call | solution.py:398
Async XLA Ops:
  1.3 0.9 %copy-start = (f32[2,128,128]{2,1,0:T(8,128)S(1)}, f32[2,128,128]{2,1,0:T(8,128)}, u32[]{:S(2)}) copy-start(f32[2,128,128]{2,1,0:T(8,128)} %constant.4.clone.rows_ref) | copy-start | bytes 393220
  2.2 0.8 %copy-start.1 = (f32[4,2,2,8,128]{4,3,2,1,0:T(8,128)S(1)}, f32[4,2,2,8,128]{4,3,2,1,0:T(8,128)}, u32[]{:S(2)}) copy-start(f32[4,2,2,8,128]{4,3,2,1,0:T(8,128)} %constant.5.clone.turns_ref) | copy-start | bytes 196612
  3.0 0.7 %copy-start.2 = (s32[1,1,1536]{2,1,0:T(1,128)S(1)}, s32[1,1,1536]{2,1,0:T(1,128)}, u32[]{:S(2)}) copy-start(s32[1,1,1536]{2,1,0:T(1,128)} %param.7) | copy-start | bytes 18436
  3.7 0.7 %copy-start.3 = (s32[1,1,1536]{2,1,0:T(1,128)S(1)}, s32[1,1,1536]{2,1,0:T(1,128)}, u32[]{:S(2)}) copy-start(s32[1,1,1536]{2,1,0:T(1,128)} %param.8) | copy-start | bytes 18436

commit v7 on v6

--- a/solution.py
+++ b/solution.py
@@ -27,15 +27,15 @@
     return rows.astype(np.float32), np.array(turns).astype(np.float32)
 
 
-def fill_tables(table, rows_ref, turns_ref, q):
-    turns = [[turns_ref[q, odd, part] for part in range(2)] for odd in range(2)]
+def fill_tables(table, waves, q):
+    turns = [[waves[pl.ds(pl.multiple_of(2 * LANES + (4 * q + 2 * odd + part) * 8, 8), 8), :] for part in range(2)] for odd in range(2)]
 
     def step(m, carry):
         tops = [[], []]
         for part in range(2):
             at = 2 * m + part
-            rc = jnp.broadcast_to(rows_ref[0, pl.ds(at, 1), :], (8, LANES))
-            rs = jnp.broadcast_to(rows_ref[1, pl.ds(at, 1), :], (8, LANES))
+            rc = jnp.broadcast_to(waves[pl.ds(at, 1), :], (8, LANES))
+            rs = jnp.broadcast_to(waves[pl.ds(LANES + at, 1), :], (8, LANES))
             for odd in range(2):
                 turn_c, turn_s = turns[odd]
                 tops[odd].append(jnp.concatenate([rc * turn_c - rs * turn_s, rs * turn_c + rc * turn_s], axis=1))
@@ -89,7 +89,7 @@
     return jnp.concatenate([top, (value - top.astype(jnp.float32)).astype(jnp.bfloat16)], axis=axis)
 
 
-def main_kernel(fold, trace_shot, trace_rcv, traces, rows_ref, turns_ref, shot_out, rcv_out,
+def main_kernel(fold, trace_shot, trace_rcv, traces, waves, shot_out, rcv_out,
                 index, held, halves, table, hot, shot_blocks, rcv_blocks, pre_send, pre_land,
                 shot_landed, rcv_landed, index_landed,
                 pairs, totals, rcv_count, count_land,
@@ -193,7 +193,7 @@
 
     def chunk_step(t, carry):
         q = lax.rem(t + me, 4)
-        fill_tables(table, rows_ref, turns_ref, q)
+        fill_tables(table, waves, q)
         first = (lax.broadcasted_iota(jnp.int32, (1, LANES), 1) + q) == 0
         sums = [None, None]
         for b in range(slots // block):
@@ -359,7 +359,7 @@
     shot_got, rcv_got = pl.pallas_call(
         main_kernel,
         out_shape=(shape((CHIPS, OWNED, LANES), f32), shape((2, CHIPS, OWNED // 2, LANES), f32)),
-        in_specs=[pl.BlockSpec(memory_space=pltpu.SMEM), vmem, vmem, pl.BlockSpec(memory_space=pl.ANY), vmem, vmem],
+        in_specs=[pl.BlockSpec(memory_space=pltpu.SMEM), vmem, vmem, pl.BlockSpec(memory_space=pl.ANY), vmem],
         out_specs=(vmem,) * 2,
         scratch_shapes=[
             VMEM((2 * tiles, LANES), jnp.int32),
@@ -394,7 +394,7 @@
             collective_id=0, has_side_effects=True, vmem_limit_bytes=VMEM_LIMIT
         ),
         name="decompose",
-    )(fold_count, trace_shot[0], trace_rcv[0], traces[0, 0], jnp.asarray(rows_np), jnp.asarray(turns_np))
+    )(fold_count, trace_shot[0], trace_rcv[0], traces[0, 0], jnp.asarray(np.concatenate([rows_np.reshape(-1, LANES), turns_np.reshape(-1, LANES)])))
     return pl.pallas_call(
         turn_kernel,
         out_shape=(shape((LANES, bins), f32), shape((LANES, bins), f32)),

time: 58.6 us -> 57.8 us (0.986)
  local copies, waits for them, and re-layouts: 3.12 us -> 2.3 us
    unnamed x8 -> x6, local copies, waits for them, and re-layouts: 3.12 us -> 2.3 us
where the time goes in v7:
time: 57.8 us; the launch traced here: 57.6 us
  Pallas kernels  54 us (93%)
  local copies, waits for them, and re-layouts  2.3 us (4%)
  between operations  1.3 us (2%)
    pallas_call x1, Pallas kernels, shards(): pl.pallas_call(main_kernel, out_shape=(shape((CHIPS, OWNED, LANES), f32),...  52.6 us
    unnamed x6, local copies, waits for them, and re-layouts  2.3 us
    pallas_call x1, Pallas kernels, shards(): pl.pallas_call(turn_kernel, out_shape=(shape((LANES, bins), f32), shape((...  1.39 us

profile of v7, /device:TPU:1, one launch (start us, length us, event | category | flops | bytes accessed | tf_op | source)
XLA Modules:
  0.0 57.6 jit_solution(11826511873021145208)
XLA Ops:
  1.3 0.0 copy-start
  1.3 0.9 %copy-done = f32[384,128]{1,0:T(8,128)S(1)} copy-done((f32[384,128]{1,0:T(8,128)S(1)}, f32[384,128]{1,0:T(8,128)}, u32[]{:S(2)}) %copy-start) | copy-done | bytes 196632
  2.2 0.0 copy-start.1
  2.2 0.7 %copy-done.1 = s32[1,1,1536]{2,1,0:T(1,128)S(1)} copy-done((s32[1,1,1536]{2,1,0:T(1,128)S(1)}, s32[1,1,1536]{2,1,0:T(1,128)}, u32[]{:S(2)}) %copy-start.1) | copy-done | bytes 6168
  2.9 0.0 copy-start.2
  2.9 0.7 %copy-done.2 = s32[1,1,1536]{2,1,0:T(1,128)S(1)} copy-done((s32[1,1,1536]{2,1,0:T(1,128)S(1)}, s32[1,1,1536]{2,1,0:T(1,128)}, u32[]{:S(2)}) %copy-start.2) | copy-done | bytes 6168
  3.6 52.6 %decompose.1 = (f32[64,16,128]{2,1,0:T(8,128)S(1)}, f32[2,64,8,128]{3,2,1,0:T(8,128)S(1)}) custom-call(s32[1,1]{1,0:T(1,128)S(6)} %copy.7.fold, s32[1,1536]{1,0:T(1,128)S(1)} %bitcast.3, s32[1,1536]{1,0:T(1,128)S(1)} %bitcast.4, bf16[1536,2048]{1,0:T(8,128)(2,1)} %bitcast.5, f32[384,128]{1,0:T(8,128)S(1)} %copy-done), custom_call_target="tpu_custom_call" | custom-call | tf_op jit(solution)/shard_map/decompose/pallas_call | solution.py:359
  56.2 1.4 %turn.1 = (f32[128,1024]{1,0:T(8,128)}, f32[128,1024]{1,0:T(8,128)}) custom-call(f32[64,16,128]{2,1,0:T(8,128)S(1)} %get-tuple-element.4.shot_in, f32[2,64,8,128]{3,2,1,0:T(8,128)S(1)} %get-tuple-element.5.rcv_in), custom_call_target="tpu_custom_call" | custom-call | tf_op jit(solution)/shard_map/turn/pallas_call | solution.py:398
Async XLA Ops:
  1.3 0.9 %copy-start = (f32[384,128]{1,0:T(8,128)S(1)}, f32[384,128]{1,0:T(8,128)}, u32[]{:S(2)}) copy-start(f32[384,128]{1,0:T(8,128)} %constant.2.clone.waves) | copy-start | bytes 589828
  2.2 0.7 %copy-start.1 = (s32[1,1,1536]{2,1,0:T(1,128)S(1)}, s32[1,1,1536]{2,1,0:T(1,128)}, u32[]{:S(2)}) copy-start(s32[1,1,1536]{2,1,0:T(1,128)} %param.6) | copy-start | bytes 18436
  2.9 0.7 %copy-start.2 = (s32[1,1,1536]{2,1,0:T(1,128)S(1)}, s32[1,1,1536]{2,1,0:T(1,128)}, u32[]{:S(2)}) copy-start(s32[1,1,1536]{2,1,0:T(1,128)} %param.7) | copy-start | bytes 18436
